TPU v7x, 256 devices: a whole 4x4x8 slice. The times are simulated.
256 devices in a mesh: dp: 32 (over x, z), cand: 8 (over y, core).
Axes of the slice: x: 4, y: 4, z: 8, core: 2. Of those that a mesh axis runs over, the one named last changes fastest.
Arguments:
- hidden: bfloat16 [64, 32, 128, 768], P('dp', 'cand'), may hold values from -24 to 24
- attn_weight: bfloat16 [768, 3072], P('dp'), may hold values from -1 to 1
- norm_gain: float32 [768], replicated, may hold values from 0.2 to 4
- pos_bias: float32 [12, 128, 128], replicated, may hold values from -5 to 5
- score_weight: float32 [768], replicated, may hold values from -4 to 4
- pair_lengths: int32 [64, 32], P('dp', 'cand'), may hold values from 32 to 128
- labels: int32 [64, 32], P('dp', 'cand'), may hold values from 0 to 3
Outputs:
- update: float32 [768, 3072], P('dp')
- loss: float32 [64], P('dp')
All inputs are finite; a program needn't handle non-finite values.
Results may differ from a plain program's by a relative error of at most 0.017.
Values may be sent and summed in bfloat16 or wider, within the bound.
A program may use at most 128 MiB of HBM per device.

v0:
```python
import jax
import jax.numpy as jnp
from jax import lax
from jax.sharding import Mesh
from jax.sharding import PartitionSpec as P

DP = ("dp_0", "dp_1")


EPS = 1e-06


def copy_for_each(value, axis):
    count = lax.axis_size(axis)
    return lax.all_to_all(
        jnp.broadcast_to(value[None], (count, *value.shape)), axis, 0, 0, tiled=True
    )


def all_in_one(value, axis):
    leaves = jax.tree.leaves(value)
    turns = sorted(range(len(leaves)), key=lambda k: -leaves[k].size)
    width = (1, *leaves[turns[0]].shape)[-1]
    lines = [
        jnp.pad(leaves[k].reshape(-1), (0, -leaves[k].size % width)).reshape(-1, width)
        for k in turns
    ]
    both, at, found = (copy_for_each(jnp.concatenate(lines), axis), 0, {})
    for k, line in zip(turns, lines):
        slab = both[:, at : at + len(line)].reshape(len(both), -1)
        found[k] = slab[:, : leaves[k].size].reshape(-1, *leaves[k].shape)
        at += len(line)
    numbers = iter(range(len(leaves)))
    return jax.tree.map(lambda _: found[next(numbers)], value)


def combined_pairwise(pieces, combine):
    while len(jax.tree.leaves(pieces)[0]) > 1:
        pieces = jax.vmap(combine)(
            *(jax.tree.map(lambda part: part[side::2], pieces) for side in (0, 1))
        )
    return jax.tree.map(lambda part: part[0], pieces)


def merged(value, axis, combine):
    pieces = all_in_one(value, axis)
    return combined_pairwise(pieces, combine)


def own_rows(terms, axes):
    subtotal = terms.astype(jnp.bfloat16)
    for axis in axes:
        subtotal = lax.psum_scatter(subtotal, axis, scatter_dimension=0, tiled=True)
    return subtotal.astype(jnp.float32)


def over_copies(value, axis):
    return copy_for_each(value, axis).astype(jnp.float32).sum(axis=0)


def of_everyone(value, axis):
    return copy_for_each(value, axis).sum(axis=0)


def rms_rows(values, gain):
    factor = lax.rsqrt(jnp.mean(values * values, axis=-1, keepdims=True) + EPS)
    return values * factor * gain


def attend(qkv, pos_bias, pair_len):
    batch, seq, triple = qkv.shape
    width = triple // 3
    heads = pos_bias.shape[0]
    head_size = width // heads
    parts = qkv.reshape(batch, seq, 3, heads, head_size)
    logits = jnp.einsum(
        "bqhd,bkhd->bhqk", parts[:, :, 0], parts[:, :, 1], preferred_element_type=jnp.float32
    )
    logits = logits + pos_bias[None]
    valid = jnp.arange(seq, dtype=jnp.int32)[None, :] < pair_len[:, None]
    logits = jnp.where(valid[:, None, None, :], logits, -1e30)
    highest = jnp.max(logits, axis=-1, keepdims=True)
    expo = jnp.exp(logits - highest)
    probs = (expo / jnp.sum(expo, axis=-1, keepdims=True)).astype(jnp.bfloat16)
    context = jnp.einsum(
        "bhqk,bkhd->bqhd", probs, parts[:, :, 2], preferred_element_type=jnp.float32
    )
    return context.astype(jnp.bfloat16).reshape(batch, seq, width)


def score_head(pooled, score_weight):
    return jnp.sum(rms_rows(pooled, 1.0) * score_weight, axis=-1)


def shards(hidden, attn_weight, norm_gain, pos_bias, score_weight, pair_lengths, labels):
    q_local, c_local, seq, width = hidden.shape
    weights = lax.all_gather(attn_weight, DP, axis=0, tiled=True)
    tokens = hidden.reshape(q_local * c_local, seq, width)
    pair_len = pair_lengths.reshape(-1)
    values = tokens.astype(jnp.float32)
    normed = rms_rows(values, norm_gain).astype(jnp.bfloat16)
    flat_norm = normed.reshape(-1, width)
    qkv = jnp.dot(flat_norm, weights[:, : 3 * width], preferred_element_type=jnp.float32)
    qkv = qkv.astype(jnp.bfloat16).reshape(q_local * c_local, seq, 3 * width)
    context, attend_back = jax.vjp(lambda block: attend(block, pos_bias, pair_len), qkv)
    flat_ctx = context.reshape(-1, width)
    out_rows = values + jnp.dot(
        flat_ctx, weights[:, 3 * width :], preferred_element_type=jnp.float32
    ).reshape(values.shape)
    live = (jnp.arange(seq, dtype=jnp.int32)[None, :] < pair_len[:, None]).astype(jnp.float32)
    share = live / pair_len.astype(jnp.float32)[:, None]
    pooled = jnp.sum(out_rows * share[:, :, None], axis=1)
    flat_scores, head_back = jax.vjp(lambda vector: score_head(vector, score_weight), pooled)
    scores = flat_scores.reshape(q_local, c_local)
    target = jnp.exp(labels.astype(jnp.float32))
    local_max = jnp.max(scores, axis=1)
    local_sum = jnp.sum(jnp.exp(scores - local_max[:, None]), axis=1)

    def combine(first, second):
        larger = jnp.maximum(first[0], second[0])
        summed = first[1] * jnp.exp(first[0] - larger) + second[1] * jnp.exp(second[0] - larger)
        return (larger, summed, first[2] + second[2], first[3] + second[3])

    highest, expsum, target_sum, target_dot = merged(
        (local_max, local_sum, jnp.sum(target, axis=1), jnp.sum(target * scores, axis=1)),
        "cand",
        combine,
    )
    loss = highest + jnp.log(expsum) - target_dot / target_sum
    score_grad = jnp.exp(scores - highest[:, None]) / expsum[:, None] - target / target_sum[:, None]
    pooled_grad = head_back(score_grad.reshape(-1))[0]
    out_grad = (pooled_grad[:, None, :] * share[:, :, None]).astype(jnp.bfloat16)
    flat_out = out_grad.reshape(-1, width)
    context_grad = jnp.dot(flat_out, weights[:, 3 * width :].T, preferred_element_type=jnp.float32)
    context_grad = context_grad.astype(jnp.bfloat16).reshape(context.shape)
    qkv_grad = attend_back(context_grad)[0].reshape(-1, 3 * width)
    dims = (((0,), (0,)), ((), ()))
    first = lax.dot_general(flat_norm, qkv_grad, dims, preferred_element_type=jnp.float32)
    second = lax.dot_general(flat_ctx, flat_out, dims, preferred_element_type=jnp.float32)
    shard = own_rows(jnp.concatenate([first, second], axis=1), DP)
    shard = over_copies(shard.astype(jnp.bfloat16), "cand").astype(jnp.float32)
    squares = of_everyone(jnp.sum(shard * shard), DP)
    rms_value = jnp.sqrt(squares / (4.0 * width * width))
    update = shard / (rms_value + EPS)
    return (update, loss)


def solution(mesh):
    split = Mesh(mesh.devices.reshape(4, 8, mesh.shape["cand"]), ("dp_0", "dp_1", "cand"))
    placed = (P(DP, "cand", None, None), P(DP, None), P(), P(), P(), P(DP, "cand"), P(DP, "cand"))
    return jax.shard_map(
        shards, mesh=split, in_specs=placed, out_specs=(P(DP, None), P(DP)), check_vma=False
    )
```

profile of v0, /device:TPU:1, one launch (start us, length us, event | category | flops | bytes accessed | tf_op | source)
XLA Modules:
  0.0 328.8 jit_solution(15862211216064773710)
XLA Ops:
  7.2 0.7 all-gather.2.cloned.1.call-update
  7.9 0.8 lt.33
  8.7 1.4 copy.102
  10.1 2.1 multiply_reduce_fusion
  12.3 1.6 multiply_convert_fusion.1
  13.9 1.6 fusion.13
  15.5 78.1 %all-gather.2.cloned.1.call-done = bf16[768,3072]{1,0:T(8,128)(2,1)} async-done(((bf16[24,3072]{1,0:T(8,128)(2,1)}), bf16[768,3072]{1,0:T(8,128)(2,1)}) %all-gather.2.cloned.1.call-update) | async-done | bytes 4718608 | tf_op jit(solution)/shard_map/all_gather | solution.py:97
  93.6 8.4 %convolution_convert_fusion = bf16[1024,2304]{1,0:T(8,128)(2,1)} fusion(bf16[1024,768]{1,0:T(8,128)(2,1)} %fusion.13, bf16[768,3072]{1,0:T(8,128)(2,1)} %all-gather.2.cloned.1.call-done), kind=kOutput, calls=%fused_computation.11 | convolution fusion | flops 3626237952 | bytes 9830400 | tf_op jit(solution)/shard_map/dot_general | solution.py:103
  102.0 7.2 %copy.98 = bf16[1024,2304]{0,1:T(8,128)(2,1)} copy(bf16[1024,2304]{1,0:T(8,128)(2,1)} %convolution_convert_fusion) | data formatting | bytes 9437184 | tf_op jit(solution)/shard_map/convert_element_type | solution.py:104
  109.2 3.6 %copy.130 = bf16[288,8,8,128]{3,2,1,0:T(8,128)(2,1)S(1)} copy(bf16[288,8,8,128]{3,1,2,0:T(8,128)(2,1)} %bitcast.103) | data formatting | bytes 9437184
  112.8 0.5 fusion.49
  113.3 1.9 fusion.5
  115.3 2.1 fusion.39
  117.4 0.5 copy-done
  117.9 5.5 %convert_reduce_fusion = (f32[8,12,128]{2,1,0:T(8,128)S(1)}, pred[8,12,128,128]{2,3,1,0:T(32,128)(4,1)}, bf16[8,12,128,128]{2,3,1,0:T(8,128)(2,1)S(1)}) fusion(f32[8,12,128]{2,1,0:T(8,128)S(1)} %get-tuple-element.25, f32[8,12,128,128]{2,3,1,0:T(8,128)S(1)} %get-tuple-element.26, f32[12,128,128]{1,2,0:T(8,128)} %copy-done.1, ...), kind=kLoop, calls=%fused_computation.7 | loop fusion | flops 12570624 | bytes 11944960 | tf_op jit(solution)/shard_map/jvp()/reduce_sum | solution.py:82
  123.4 0.9 convolution_convert_fusion.5
  124.4 0.4 copy-done.4
  124.9 3.0 fusion.15
  128.7 0.6 broadcast_in_dim.40
  129.3 8.7 %all-to-all-start = ((f32[8,4,2]{1,2,0:T(2,128)}), f32[8,4,2]{1,2,0:T(2,128)S(1)}, u32[]{:S(2)}, u32[]{:S(2)}) async-start(f32[8,4,2]{1,2,0:T(2,128)} %broadcast_in_dim.40), calls=%async_computation | async-start | bytes 16384 | tf_op jit(solution)/shard_map/all_to_all | solution.py:15
  138.2 3.8 %copy.116 = bf16[8,128,12,64]{1,0,3,2:T(8,128)(2,1)} copy(bf16[8,128,12,64]{1,3,2,0:T(8,128)(2,1)} %bitcast.106) | data formatting | bytes 3145728 | tf_op jit(solution)/shard_map/jvp()/convert_element_type | solution.py:88
  142.0 0.6 all-to-all-done
  144.9 0.2 fusion.11
  145.1 3.9 %convolution_convert_fusion.4 = bf16[1024,768]{1,0:T(8,128)(2,1)} fusion(bf16[1024,768]{1,0:T(8,128)(2,1)S(1)} %fusion.11, bf16[768,3072]{1,0:T(8,128)(2,1)} %all-gather.2.cloned.1.call-done), kind=kOutput, calls=%fused_computation.44 | convolution fusion | flops 1208745984 | bytes 4325376 | tf_op jit(solution)/shard_map/dot_general | solution.py:134
  149.0 2.6 copy.109
  151.6 2.0 copy.131
  153.6 2.2 fusion.30
  155.8 5.2 %fusion.3 = (f32[8,12,128]{2,1,0:T(8,128)S(1)}, bf16[8,12,128,128]{2,3,1,0:T(8,128)(2,1)S(1)}) fusion(f32[8,12,128]{2,1,0:T(8,128)S(1)} %multiply_divide_fusion, f32[8,12,128]{2,1,0:T(8,128)S(1)} %get-tuple-element.25, f32[8,12,128,128]{2,3,1,0:T(8,128)} %copy-done, f32[12,128,128]{1,2,0:T(8,128)S(1)} %copy-done.2, pred[8,128]{1,0:T(8,128)(4,1)S(1)} %iota_compare_fusion, ...), kind=kOutput, calls=%fused_computation.5 | convolution fusion | flops 213897216 | bytes 13517824 | tf_op jit(solution)/shard_map/transpose(jvp(bhqk,bkhd->bqhd))/dot_general | solution.py:85
  161.2 3.1 fusion.46
  164.3 2.6 fusion.32
  166.9 1.5 fusion.31
  168.6 0.6 pad_add_fusion
  169.2 9.3 %copy.115 = bf16[8,128,3,12,64]{1,0,4,3,2:T(8,128)(2,1)S(1)} copy(bf16[8,128,3,12,64]{1,4,3,0,2:T(8,128)(2,1)S(1)} %pad_add_fusion) | data formatting | bytes 9437184 | tf_op jit(solution)/shard_map/transpose(jvp())/add_any | solution.py:77
  178.5 4.4 %convolution_convert_fusion.1 = bf16[768,2304]{1,0:T(8,128)(2,1)S(1)} fusion(bf16[1024,768]{1,0:T(8,128)(2,1)S(1)} %bitcast.110, bf16[288,8,8,128]{3,2,1,0:T(8,128)(2,1)S(1)} %bitcast.109), kind=kOutput, calls=%fused_computation.12 | convolution fusion | flops 3625648128 | bytes 9830400 | tf_op jit(solution)/shard_map/dot_general | solution.py:138
  182.9 1.4 fusion.27
  184.3 2.8 pad_maximum_fusion
  187.2 50.1 %reduce-scatter.3.cloned.1.call-done = bf16[192,3072]{1,0:T(8,128)(2,1)} async-done(((bf16[768,3072]{1,0:T(8,128)(2,1)}), bf16[192,3072]{1,0:T(8,128)(2,1)}) %reduce-scatter.3.cloned.1.call-update) | async-done | bytes 1179664 | tf_op jit(solution)/shard_map/reduce_scatter | solution.py:53
  237.3 37.3 %reduce-scatter.5.cloned.1.call-done = bf16[24,3072]{1,0:T(8,128)(2,1)} async-done(((bf16[192,3072]{1,0:T(8,128)(2,1)}), bf16[24,3072]{1,0:T(8,128)(2,1)}) %reduce-scatter.5.cloned.1.call-update) | async-done | bytes 147472 | tf_op jit(solution)/shard_map/reduce_scatter | solution.py:53
  274.6 2.0 broadcast_in_dim.85
  276.7 9.4 %all-to-all-start.1 = ((bf16[8,24,3072]{2,1,0:T(8,128)(2,1)}), bf16[8,24,3072]{2,1,0:T(8,128)(2,1)S(1)}, u32[]{:S(2)}, u32[]{:S(2)}) async-start(bf16[8,24,3072]{2,1,0:T(8,128)(2,1)} %broadcast_in_dim.85), calls=%async_computation.3 | async-start | bytes 2359296 | tf_op jit(solution)/shard_map/all_to_all | solution.py:15
  286.8 15.7 %all-to-all-done.1 = bf16[8,24,3072]{2,1,0:T(8,128)(2,1)S(1)} async-done(((bf16[8,24,3072]{2,1,0:T(8,128)(2,1)}), bf16[8,24,3072]{2,1,0:T(8,128)(2,1)S(1)}, u32[]{:S(2)}, u32[]{:S(2)}) %all-to-all-start.1) | async-done | bytes 1179680 | tf_op jit(solution)/shard_map/all_to_all | solution.py:15
  302.6 0.7 multiply_reduce_fusion.1
  303.3 1.3 broadcast_in_dim.86
  304.5 6.8 %all-to-all-start.2 = ((f32[32,1,1]{2,1,0:T(1,128)}), f32[32,1,1]{2,1,0:T(1,128)S(1)}, u32[]{:S(2)}, u32[]{:S(2)}) async-start(f32[32,1,1]{2,1,0:T(1,128)} %broadcast_in_dim.86), calls=%async_computation.4 | async-start | bytes 32768 | tf_op jit(solution)/shard_map/all_to_all | solution.py:15
  311.4 0.5 divide_subtract_fusion.1
  311.9 8.1 %all-to-all-done.2 = f32[32,1,1]{2,1,0:T(1,128)S(1)} async-done(((f32[32,1,1]{2,1,0:T(1,128)}), f32[32,1,1]{2,1,0:T(1,128)S(1)}, u32[]{:S(2)}, u32[]{:S(2)}) %all-to-all-start.2) | async-done | bytes 160 | tf_op jit(solution)/shard_map/all_to_all | solution.py:15
  320.0 0.6 reduce_sum.161
  321.3 0.7 broadcast_divide_fusion
  (95 shorter events, 4.7 us)
Async XLA Ops:
  7.2 5.2 %copy-start.3 = (bf16[2,4,128,768]{3,2,1,0:T(8,128)(2,1)S(1)}, bf16[2,4,128,768]{3,2,1,0:T(8,128)(2,1)}, u32[]{:S(2)}) copy-start(bf16[2,4,128,768]{3,2,1,0:T(8,128)(2,1)} %param.7) | copy-start | bytes 4718596
  7.2 5.2 %copy-start.16 = (f32[768]{0:T(1024)S(1)}, f32[768]{0:T(1024)}, u32[]{:S(2)}) copy-start(f32[768]{0:T(1024)} %param.9) | copy-start | bytes 9220
  7.2 86.4 %all-gather.2.cloned.1.call-start = ((), (), s32[]{:S(2)}) async-start(), calls=%async_computation.5 | async-start | bytes 4866048 | tf_op jit(solution)/shard_map/all_gather | solution.py:97
  10.1 105.2 %copy-start.1 = (f32[12,128,128]{1,2,0:T(8,128)}, f32[12,128,128]{1,2,0:T(8,128)S(1)}, u32[]{:S(2)}) copy-start(f32[12,128,128]{1,2,0:T(8,128)S(1)} %copy.102) | copy-start | bytes 2359300
  113.3 2.0 copy-start.5
  113.3 2.0 copy-start.7
  113.3 10.1 %copy-start.10 = (bf16[8,128,1,12,64]{1,0,4,3,2:T(8,128)(2,1)}, bf16[8,128,1,12,64]{1,0,4,3,2:T(8,128)(2,1)S(1)}, u32[]{:S(2)}) copy-start(bf16[8,128,1,12,64]{1,0,4,3,2:T(8,128)(2,1)S(1)} %get-tuple-element.16) | copy-start | bytes 4718596
  115.3 2.7 copy-start
  123.4 1.4 copy-start.4
  124.4 3.5 %copy-start.12 = (bf16[8,12,64,128]{3,2,1,0:T(8,128)(2,1)}, bf16[8,12,64,128]{3,2,1,0:T(8,128)(2,1)S(1)}, u32[]{:S(2)}) copy-start(bf16[8,12,64,128]{3,2,1,0:T(8,128)(2,1)S(1)} %convolution_convert_fusion.5) | copy-start | bytes 4718596
  124.9 3.1 copy-start.15
  124.9 3.5 %copy-start.17 = (s32[2,4]{1,0:T(2,128)S(1)}, s32[2,4]{1,0:T(2,128)}, u32[]{:S(2)}) copy-start(s32[2,4]{1,0:T(2,128)} %param.13) | copy-start | bytes 100
  129.3 13.3 %all-to-all-start = ((f32[8,4,2]{1,2,0:T(2,128)}), f32[8,4,2]{1,2,0:T(2,128)S(1)}, u32[]{:S(2)}, u32[]{:S(2)}) async-start(f32[8,4,2]{1,2,0:T(2,128)} %broadcast_in_dim.40), calls=%async_computation | async-start | bytes 16384 | tf_op jit(solution)/shard_map/all_to_all | solution.py:15
  138.0 99.3 %reduce-scatter.3.cloned.1.call-start = ((), (), s32[]{:S(2)}) async-start(), calls=%async_computation.6 | async-start | bytes 5898240 | tf_op jit(solution)/shard_map/reduce_scatter | solution.py:53
  151.6 4.3 %copy-start.11 = (bf16[8,128,1,12,64]{1,0,4,3,2:T(8,128)(2,1)S(1)}, bf16[8,128,1,12,64]{1,0,4,3,2:T(8,128)(2,1)}, u32[]{:S(2)}) copy-start(bf16[8,128,1,12,64]{1,0,4,3,2:T(8,128)(2,1)} %copy-done.10) | copy-start | bytes 4718596
  153.5 2.3 copy-start.2
  153.5 7.6 %slice-start = ((s8[6291456]{0:T(1024)(128)(4,1)}), s8[4194304]{0:T(1024)(128)(4,1)S(1)}, s32[]{:S(2)}) async-start(s8[6291456]{0:T(1024)(128)(4,1)} %bitcast.100), calls=%async_computation.8 | async-start | bytes 8388608
  155.8 5.3 %slice-start.1 = ((s8[6291456]{0:T(1024)(128)(4,1)}), s8[2097152]{0:T(1024)(128)(4,1)S(1)}, s32[]{:S(2)}) async-start(s8[6291456]{0:T(1024)(128)(4,1)} %bitcast.100), calls=%async_computation.9 | async-start | bytes 4194304
  161.1 3.1 copy-start.8
  161.1 3.1 copy-start.9
  164.3 2.6 copy-start.6
  169.2 9.3 %copy-start.13 = (bf16[2,4,128,768]{3,2,1,0:T(8,128)(2,1)S(1)}, bf16[2,4,128,768]{3,2,1,0:T(8,128)(2,1)}, u32[]{:S(2)}) copy-start(bf16[2,4,128,768]{3,2,1,0:T(8,128)(2,1)} %multiply_convert_fusion.1) | copy-start | bytes 4718596
  178.5 4.4 %copy-start.14 = (bf16[8,128,12,64]{1,0,3,2:T(8,128)(2,1)S(1)}, bf16[8,128,12,64]{1,0,3,2:T(8,128)(2,1)}, u32[]{:S(2)}) copy-start(bf16[8,128,12,64]{1,0,3,2:T(8,128)(2,1)} %copy.116) | copy-start | bytes 4718596
  187.1 87.5 %reduce-scatter.5.cloned.1.call-start = ((), (), s32[]{:S(2)}) async-start(), calls=%async_computation.7 | async-start | bytes 1327104 | tf_op jit(solution)/shard_map/reduce_scatter | solution.py:53
  276.7 25.8 %all-to-all-start.1 = ((bf16[8,24,3072]{2,1,0:T(8,128)(2,1)}), bf16[8,24,3072]{2,1,0:T(8,128)(2,1)S(1)}, u32[]{:S(2)}, u32[]{:S(2)}) async-start(bf16[8,24,3072]{2,1,0:T(8,128)(2,1)} %broadcast_in_dim.85), calls=%async_computation.3 | async-start | bytes 2359296 | tf_op jit(solution)/shard_map/all_to_all | solution.py:15
  304.5 15.4 %all-to-all-start.2 = ((f32[32,1,1]{2,1,0:T(1,128)}), f32[32,1,1]{2,1,0:T(1,128)S(1)}, u32[]{:S(2)}, u32[]{:S(2)}) async-start(f32[32,1,1]{2,1,0:T(1,128)} %broadcast_in_dim.86), calls=%async_computation.4 | async-start | bytes 32768 | tf_op jit(solution)/shard_map/all_to_all | solution.py:15
Sparse Core Ops, SparseCore 0:
  10.6 82.9 all-gather.1
  187.3 49.9 reduce-scatter.2
  239.8 34.7 reduce-scatter.4
where the time goes:
time: 333 us; the launch traced here: 329 us
  waiting for transfers between devices  191 us (57%)
  local copies, waits for them, and re-layouts  38.1 us (11%)
  matrix products  35.5 us (11%)
  starting transfers between devices  25.2 us (8%)
  other arithmetic  24.2 us (7%)
  between operations  15.2 us (5%)
    reduce_scatter x2, waiting for transfers between devices, own_rows(): subtotal = lax.psum_scatter(subtotal, axis, scatter_dimension=0, tiled=True)  87.4 us
    all_gather x1, waiting for transfers between devices, shards(): weights = lax.all_gather(attn_weight, DP, axis=0, tiled=True)  78.1 us
    all_to_all x3, starting transfers between devices, copy_for_each(): lax.all_to_all(jnp.broadcast_to(value[None], (count, *value.shape)), axis...  24.9 us
    all_to_all x3, waiting for transfers between devices, copy_for_each(): lax.all_to_all(jnp.broadcast_to(value[None], (count, *value.shape)), axis...  24.4 us
    add_any x1, local copies, waits for them, and re-layouts, attend(): parts[:, :, 0]  9.26 us
    dot_general x3, matrix products, attend(): jnp.einsum('bhqk,bkhd->bqhd', probs, parts[:, :, 2], preferred_element_ty...  8.43 us
    dot_general x1, matrix products, shards(): jnp.dot(flat_norm, weights[:, :3 * width], preferred_element_type=jnp.flo...  8.43 us
    unnamed x43, local copies, waits for them, and re-layouts  7.97 us
  transfers between devices with their start and end apart: 6, of which 6 were waited for; matrix products, arithmetic and copies ran while one was open for 4% of the time, Pallas kernels for 0%

commit v1 on v0

v1 whole, which is shorter than its diff:
```python
import functools

import jax
import jax.numpy as jnp
from jax import lax
from jax.experimental import pallas as pl
from jax.experimental.pallas import tpu as pltpu
from jax.sharding import Mesh
from jax.sharding import PartitionSpec as P

EPS = 1e-06
MESH = pl.DeviceIdType.MESH
F32, BF16 = jnp.float32, jnp.bfloat16
NEG = -1e30
PARTS = 3
LANES = 128


def dot(a, b, ca=1, cb=0):
    return lax.dot_general(a, b, (((ca,), (cb,)), ((), ())), preferred_element_type=F32)


def iota(shape, axis):
    return lax.broadcasted_iota(jnp.int32, shape, axis)


def step_kernel(dims, hid, wsh, gain, bias, sw, lens, labs, upd, loss, norm, norm_t, w, qk, prob, grad, hsum, svec, avec, uvec, dqk,
                zbuf, exb, r0, a1, a1s, b1, b1s, a2, b2, zs, z3, ob, sq,
                zsem, xsem, fsem, dsem, esem, r0sem, a1sem, b1sem, a2sem, b2sem, z3sem, obsem, sqsem):
    X, Z, Y, C = dims
    QL, CL, T, D = hid.shape
    H = bias.shape[0]
    HP = H // 2
    NP = QL * CL
    R = wsh.shape[0]
    XR = Z * R
    HR = XR // 2
    ZH = Z // 2
    NC = 4 * D // PARTS // C
    NB = NC // Y
    x, z, y, c = (lax.axis_index(name) for name in ("x", "z", "y", "c"))
    other = 1 - c
    cand = y * C + c
    started = []

    def at_x(d):
        return {"x": lax.rem(x + d, X)}

    def at_z(d):
        return {"z": lax.rem(z + d, Z)}

    def at_y(d):
        return {"y": lax.rem(y + d, Y)}

    def at_cand(i):
        return {"y": lax.rem(y + i // C, Y), "c": lax.rem(c + i % C, C)}

    def at_dp(i):
        return {"x": lax.rem(x + i // Z, X), "z": lax.rem(z + lax.rem(i, Z), Z)}

    def put(src, dst, sems, to):
        copy = pltpu.make_async_remote_copy(src, dst, sems.at[0], sems.at[1], device_id=to, device_id_type=MESH)
        copy.start()
        started.append(copy)
        return copy

    def cols(n, width):
        return pl.ds(pl.multiple_of(n, LANES), width)

    bar = pltpu.get_barrier_semaphore()

    def greet_dp(i, carry):
        pl.semaphore_signal(bar, 1, device_id=at_dp(i), device_id_type=MESH)
        return carry

    lax.fori_loop(1, X * Z, greet_dp, 0)
    for i in range(1, Y * C):
        pl.semaphore_signal(bar, 1, device_id=at_cand(i), device_id_type=MESH)

    def pair_len(p):
        return lens[p // CL, lax.rem(p, CL)]

    def normalise(p, carry):
        v = hid[p // CL, lax.rem(p, CL)].astype(F32)
        n = v * lax.rsqrt(jnp.mean(v * v, axis=1, keepdims=True) + EPS) * gain[...]
        rows = pl.ds(pl.multiple_of(p * T, T), T)
        norm[rows, :] = n.astype(BF16)
        norm_t[:, cols(p * T, T)] = n.T.astype(BF16)
        live = iota((T, 1), 0) < pair_len(p)
        hsum[pl.ds(p, 1), :] = jnp.sum(jnp.where(live, v, 0.0), axis=0, keepdims=True)
        return carry

    lax.fori_loop(0, NP, normalise, 0)
    pl.semaphore_wait(bar, X * Z - 1 + Y * C - 1)

    def part_cols(g, core):
        return cols((2 * g + core) * D, D)

    zcopies = {}
    for g in (0, 1):
        for d in range(1, Z):
            zcopies[g, d] = put(wsh.at[:, part_cols(g, c)], zbuf.at[g, z], zsem.at[g, d], at_z(d))
        zbuf[g, z] = wsh[:, part_cols(g, c)]

    def rows_of(d, lo=0, n=XR):
        return pl.ds(pl.multiple_of(lax.rem(x + d + X, X) * XR + lo, HR), n)

    near = [1] if X == 2 else [1, X - 1]
    xcopies, fcopies, dcopies = {}, {}, {}

    def gather_first(g):
        for d in range(1, Z):
            zcopies[g, d].wait_recv()
        for k in range(0, D, 256):
            blk = zbuf[g, :, :, k : k + 256].astype(F32).reshape(XR, 256).astype(BF16)
            w[rows_of(0), cols((2 * g + c) * D + k, 256)] = blk
        own = w.at[rows_of(0), part_cols(g, c)]
        for d in near:
            xcopies[g, d] = put(own, own, xsem.at[g, d], at_x(d))
        dcopies[g, 0] = put(own, own, dsem.at[g, 0], {"c": other})

    def gather_second(g):
        for d in near:
            xcopies[g, d].wait_recv()
            if X == 4:
                half = w.at[rows_of(-d, 0 if d == 1 else HR, HR), part_cols(g, c)]
                fcopies[g, d] = put(half, half, fsem.at[g, d], at_x(d))
            blk = w.at[rows_of(-d), part_cols(g, c)]
            dcopies[g, d] = put(blk, blk, dsem.at[g, d], {"c": other})

    def gather_third(g):
        if X == 4:
            for d in near:
                fcopies[g, d].wait_recv()
            blk = w.at[rows_of(2), part_cols(g, c)]
            dcopies[g, 2] = put(blk, blk, dsem.at[g, 2], {"c": other})

    def gather_last(g):
        for d in range(X):
            dcopies[g, d].wait_recv()

    gather_first(0)
    gather_second(0)
    gather_third(0)
    gather_first(1)
    gather_last(0)

    for n in range(0, 2 * D, 256):
        qk[:, n : n + 256] = dot(norm[...], w[:, n : n + 256]).astype(BF16)
    gather_second(1)

    half_lane = iota((1, LANES), 1) < LANES // 2
    ones = [jnp.where(half_lane, 1.0, 0.0).astype(BF16), jnp.where(half_lane, 0.0, 1.0).astype(BF16)]

    def both(v):
        return jnp.concatenate([v * ones[0], v * ones[1]], axis=0)

    svec[...] = jnp.zeros_like(svec)

    def attend(p, carry):
        rows = pl.ds(pl.multiple_of(p * T, T), T)
        n_live = pair_len(p)
        live_key = iota((1, T), 1) < n_live
        live_row = iota((T, 1), 0) < n_live
        for h in range(HP):
            q2 = qk[rows, h * LANES : (h + 1) * LANES]
            k2 = qk[rows, D + h * LANES : D + (h + 1) * LANES]
            s = dot(both(q2), k2, 1, 1) + bias[2 * h : 2 * h + 2].reshape(2 * T, T)
            s = jnp.where(live_key, s, NEG)
            e = jnp.exp(s - jnp.max(s, axis=1, keepdims=True))
            pr = (e * (1.0 / jnp.sum(e, axis=1, keepdims=True))).astype(BF16)
            prob[p, h] = pr
            for k in (0, 1):
                pk = jnp.where(live_row, pr[k * T : (k + 1) * T].astype(F32), 0.0)
                svec[p, 2 * h + k : 2 * h + k + 1, :] = jnp.sum(pk, axis=0, keepdims=True)
        a = dot(svec[p].astype(BF16), norm[rows, :])
        avec[pl.ds(pl.multiple_of(p * 16, 16), 16), :] = a.astype(BF16)
        return carry

    lax.fori_loop(0, NP, attend, 0)
    gather_third(1)
    gather_last(1)

    wv = w.at[:, 2 * D : 3 * D]
    wo = w.at[:, 3 * D : 4 * D]
    head_of = (iota((16, D), 1) // (D // H)) == iota((16, D), 0)
    prow = iota((NP, 1), 0)
    length, target = jnp.zeros((NP, 1), F32), jnp.zeros((NP, 1), F32)
    for p in range(NP):
        length = jnp.where(prow == p, lens[p // CL, p % CL].astype(F32), length)
        target = jnp.where(prow == p, labs[p // CL, p % CL].astype(F32), target)
    inv_len = 1.0 / length
    target = jnp.exp(target)

    zv = dot(avec[...], wv[...]).reshape(NP, 16, D)
    csum = jnp.sum(jnp.where(head_of[None], zv, 0.0), axis=1)
    pooled = hsum[...] * inv_len + dot((csum * inv_len).astype(BF16), wo[...])
    factor = lax.rsqrt(jnp.mean(pooled * pooled, axis=1, keepdims=True) + EPS)
    score = jnp.sum(pooled * factor * sw[...], axis=1, keepdims=True)

    exb[cand, 0] = jnp.broadcast_to(score, (NP, LANES))
    exb[cand, 1] = jnp.broadcast_to(target, (NP, LANES))
    ecopies = [put(exb.at[cand], exb.at[cand], esem.at[i], at_cand(i)) for i in range(1, Y * C)]
    for copy in ecopies:
        copy.wait_recv()
    scores, targets = exb[:, 0], exb[:, 1]
    query = iota((NP, LANES), 0) // CL

    def per_query(v, op, neutral):
        out = v
        for k in range(QL):
            out = jnp.where(query == k, op(jnp.where(query == k, v, neutral), axis=0, keepdims=True), out)
        return out

    highest = per_query(jnp.max(scores, axis=0), jnp.max, -jnp.inf)
    expsum = per_query(jnp.sum(jnp.exp(scores - highest[None]), axis=0), jnp.sum, 0.0)
    target_sum = per_query(jnp.sum(targets, axis=0), jnp.sum, 0.0)
    target_dot = per_query(jnp.sum(targets * scores, axis=0), jnp.sum, 0.0)
    loss[...] = highest + jnp.log(expsum) - target_dot / target_sum
    sgrad = (jnp.exp(score - highest) / expsum - target / target_sum)[:, :1]

    along = jnp.sum(pooled * sw[...], axis=1, keepdims=True) * (1.0 / D)
    pooled_grad = sgrad * (factor * sw[...] - pooled * (factor * factor * factor * along))
    g = (pooled_grad * inv_len).astype(BF16)
    cg = dot(g, wo[...], 1, 1)
    cexp = jnp.where(head_of[None], cg[:, None, :], 0.0).reshape(NP * 16, D).astype(BF16)
    tv = dot(cexp, wv[...], 1, 1).astype(BF16)
    for p in range(NP):
        uvec[p] = dot(tv[p * 16 : (p + 1) * 16], norm_t[:, p * T : (p + 1) * T])

    def keep(n, value):
        grad[:, :, n : n + value.shape[1]] = value.astype(BF16).reshape(X, XR, value.shape[1])

    csum_b = csum.astype(BF16)
    for n in range(0, D, 256):
        keep(n, dot(csum_b, g[:, n : n + 256], 0, 0))
    for n in range(0, D, 256):
        keep(D + n, dot(avec[...], cexp[:, n : n + 256], 0, 0))

    r0c, a1c, b1c, a2c, b2c, z3c, obc = {}, {}, {}, {}, {}, {}, {}

    def mine(t):
        return cols((t * C + c) * NC, NC)

    def reduce_0(t):
        r0c[t] = put(grad.at[:, :, cols((t * C + other) * NC, NC)], r0.at[t], r0sem.at[t], {"c": other})

    def reduce_1(t):
        r0c[t].wait_recv()
        r0[t] = (r0[t].astype(F32) + grad[:, :, mine(t)].astype(F32)).astype(BF16)
        for d in range(1, X):
            a1c[t, d] = put(r0.at[t, lax.rem(x + d, X), :HR, :], a1.at[t, d - 1], a1sem.at[t, d], at_x(d))
        for d in range(1, Y):
            to = cols(lax.rem(y + d, Y) * NB, NB)
            b1c[t, d] = put(r0.at[t, :, HR:, to], b1.at[t, d - 1], b1sem.at[t, d], at_y(d))

    def reduce_2(t):
        total = r0[t, x, :HR, :].astype(F32)
        for d in range(1, X):
            a1c[t, d].wait_recv()
            total += a1[t, d - 1].astype(F32)
        a1s[t] = total.astype(BF16)
        total = r0[t, :, HR:, cols(y * NB, NB)].astype(F32)
        for d in range(1, Y):
            b1c[t, d].wait_recv()
            total += b1[t, d - 1].astype(F32)
        b1s[t] = total.astype(BF16)
        for d in range(1, Y):
            a2c[t, d] = put(a1s.at[t, :, cols(lax.rem(y + d, Y) * NB, NB)], a2.at[t, d - 1], a2sem.at[t, d], at_y(d))
        for d in range(1, X):
            b2c[t, d] = put(b1s.at[t, lax.rem(x + d, X)], b2.at[t, d - 1], b2sem.at[t, d], at_x(d))

    def reduce_3(t):
        total = a1s[t, :, cols(y * NB, NB)].astype(F32)
        for d in range(1, Y):
            a2c[t, d].wait_recv()
            total += a2[t, d - 1].astype(F32)
        zs[t, :ZH] = total.reshape(ZH, R, NB).astype(BF16)
        total = b1s[t, x].astype(F32)
        for d in range(1, X):
            b2c[t, d].wait_recv()
            total += b2[t, d - 1].astype(F32)
        zs[t, ZH:] = total.reshape(ZH, R, NB).astype(BF16)
        for d in range(1, Z):
            z3c[t, d] = put(zs.at[t, lax.rem(z + d, Z)], z3.at[t, d - 1], z3sem.at[t, d], at_z(d))

    def reduce_4(t):
        total = zs[t, z].astype(F32)
        for d in range(1, Z):
            z3c[t, d].wait_recv()
            total += z3[t, d - 1].astype(F32)
        ob[t, cand] = total.astype(BF16)
        for i in range(1, Y * C):
            obc[t, i] = put(ob.at[t, cand], ob.at[t, cand], obsem.at[t, i], at_cand(i))

    def backward(h, carry):
        for p in range(NP):
            n_live = lens[p // CL, p % CL]
            live_row = iota((T, 1), 0) < n_live
            q2 = qk[p * T : (p + 1) * T, cols(h * LANES, LANES)]
            k2 = qk[p * T : (p + 1) * T, cols(D + h * LANES, LANES)]
            pr = prob[p, h].astype(F32).reshape(2, T, T)
            ds = []
            for k in (0, 1):
                pu = pr[k] * uvec[p, pl.ds(2 * h + k, 1), :]
                mean = jnp.sum(pu, axis=1, keepdims=True)
                ds.append(jnp.where(live_row, pu - pr[k] * mean, 0.0).astype(BF16))
            dqk[p * T : (p + 1) * T, :LANES] = dot(jnp.concatenate(ds, axis=1), both(k2)).astype(BF16)
            dqk[p * T : (p + 1) * T, LANES:] = dot(jnp.concatenate(ds, axis=0), both(q2), 0, 0).astype(BF16)
        dw = dot(norm_t[...], dqk[...]).astype(BF16)
        grad[:, :, cols(2 * D + h * 2 * LANES, 2 * LANES)] = dw.reshape(X, XR, 2 * LANES)
        return carry

    reduce_0(0)
    lax.fori_loop(0, 2, backward, 0)
    reduce_0(1)
    reduce_1(0)
    lax.fori_loop(2, 4, backward, 0)
    reduce_1(1)
    reduce_2(0)
    lax.fori_loop(4, HP, backward, 0)
    reduce_0(2)
    reduce_2(1)
    reduce_3(0)
    reduce_1(2)
    reduce_3(1)
    reduce_4(0)
    reduce_2(2)
    reduce_4(1)
    reduce_3(2)
    reduce_4(2)
    for copy in obc.values():
        copy.wait_recv()

    me = x * Z + z
    squares = jnp.zeros((R, NB), F32)
    for t in range(PARTS):
        for k in range(Y * C):
            v = ob[t, k].astype(F32)
            squares += v * v
    tile = squares.reshape(R // 8, 8, NB // LANES, LANES) if NB > LANES else squares.reshape(R // 8, 8, LANES)
    tile = jnp.sum(tile, axis=(0, 2)) if NB > LANES else jnp.sum(tile, axis=0)
    sq[me] = tile

    def sq_copy(i):
        return pltpu.make_async_remote_copy(
            sq.at[me], sq.at[me], sqsem.at[0, i], sqsem.at[1, i], device_id=at_dp(i), device_id_type=MESH
        )

    def sq_start(i, carry):
        sq_copy(i).start()
        return carry

    def sq_wait(i, carry):
        sq_copy(i).wait()
        return carry

    lax.fori_loop(1, X * Z, sq_start, 0)
    lax.fori_loop(1, X * Z, sq_wait, 0)
    everything = jnp.sum(sq[...], axis=0)
    everything = jnp.sum(jnp.sum(everything, axis=1, keepdims=True), axis=0, keepdims=True)
    scale = 1.0 / (jnp.sqrt(everything * (1.0 / (4.0 * D * D))) + EPS)
    for t in range(PARTS):
        for k in range(Y * C):
            for m in range(NB // LANES):
                b = ((t * C + k % C) * NC + (k // C) * NB) // LANES + m
                if b < HP:
                    n = 3 * D + b * LANES
                elif b < 2 * HP:
                    n = 2 * D + (b - HP) * LANES
                else:
                    n = (b - 2 * HP) % 2 * D + (b - 2 * HP) // 2 * LANES
                upd[:, n : n + LANES] = ob[t, k, :, m * LANES : (m + 1) * LANES].astype(F32) * scale
    for copy in started:
        copy.wait_send()


def solution(mesh):
    n_dp, n_cand = mesh.shape["dp"], mesh.shape["cand"]
    X, C = (4 if n_dp == 32 else 2), 2
    Z, Y = n_dp // X, n_cand // C
    split = Mesh(mesh.devices.reshape(X, Z, Y, C), ("x", "z", "y", "c"))
    dp, cand = ("x", "z"), ("y", "c")

    def shards(hidden, attn_weight, norm_gain, pos_bias, score_weight, pair_lengths, labels):
        QL, CL, T, D = hidden.shape
        H = pos_bias.shape[0]
        R = attn_weight.shape[0]
        NP, XR, NC = QL * CL, Z * R, 4 * D // PARTS // C
        HR, NB = XR // 2, NC // Y
        vmem, smem = pl.BlockSpec(memory_space=pltpu.VMEM), pl.BlockSpec(memory_space=pltpu.SMEM)
        dma = pltpu.SemaphoreType.DMA
        V = pltpu.VMEM
        update, loss = pl.pallas_call(
            functools.partial(step_kernel, (X, Z, Y, C)),
            out_shape=(jax.ShapeDtypeStruct((R, 4 * D), F32), jax.ShapeDtypeStruct((NP, LANES), F32)),
            in_specs=[vmem] * 5 + [smem] * 2,
            out_specs=(vmem, vmem),
            scratch_shapes=[
                V((NP * T, D), BF16),
                V((D, NP * T), BF16),
                V((D, 4 * D), BF16),
                V((NP * T, 2 * D), BF16),
                V((NP, H // 2, 2 * T, T), BF16),
                V((X, XR, 4 * D), BF16),
                V((NP, D), F32),
                V((NP, 16, T), F32),
                V((NP * 16, D), BF16),
                V((NP, 16, T), F32),
                V((NP * T, 2 * LANES), BF16),
                V((2, Z, R, D), BF16),
                V((Y * C, 2, NP, LANES), F32),
                V((PARTS, X, XR, NC), BF16),
                V((PARTS, X - 1, HR, NC), BF16),
                V((PARTS, HR, NC), BF16),
                V((PARTS, Y - 1, X, HR, NB), BF16),
                V((PARTS, X, HR, NB), BF16),
                V((PARTS, Y - 1, HR, NB), BF16),
                V((PARTS, X - 1, HR, NB), BF16),
                V((PARTS, Z, R, NB), BF16),
                V((PARTS, Z - 1, R, NB), BF16),
                V((PARTS, Y * C, R, NB), BF16),
                V((X * Z, 8, LANES), F32),
                dma((2, Z, 2)),
                dma((2, X, 2)),
                dma((2, X, 2)),
                dma((2, X, 2)),
                dma((Y * C, 2)),
                dma((PARTS, 2)),
                dma((PARTS, X, 2)),
                dma((PARTS, Y, 2)),
                dma((PARTS, Y, 2)),
                dma((PARTS, X, 2)),
                dma((PARTS, Z, 2)),
                dma((PARTS, Y * C, 2)),
                dma((2, X * Z)),
            ],
            compiler_params=pltpu.CompilerParams(collective_id=0, has_side_effects=True, vmem_limit_bytes=60 * 2**20),
        )(hidden, attn_weight, norm_gain[None], pos_bias, score_weight[None], pair_lengths, labels)
        return update, loss[::CL, 0]

    placed = (P(dp, cand, None, None), P(dp, None), P(), P(), P(), P(dp, cand), P(dp, cand))
    return jax.shard_map(shards, mesh=split, in_specs=placed, out_specs=(P(dp, None), P(dp)), check_vma=False)
```

time: 333 us -> 110 us (0.33); the launches traced: 329 us -> 110 us
  waiting for transfers between devices: 191 us -> 0 us
  Pallas kernels: 0 us -> 104 us
  matrix products: 35.5 us -> 0 us
  local copies, waits for them, and re-layouts: 38.1 us -> 4.94 us
  starting transfers between devices: 25.2 us -> 0 us
  other arithmetic: 24.2 us -> 0.63 us
  between operations: 15.2 us -> 0.64 us
    pallas_call x0 -> x1, Pallas kernels: none -> 104 us  [shards(): pl.pallas_call(functools.partial(step_kernel, (X, Z, Y, C)), out_shape=(j...]
    reduce_scatter x2 -> x0, waiting for transfers between devices: 87.4 us -> none  [own_rows(): subtotal = lax.psum_scatter(subtotal, axis, scatter_dimension=0, tiled=True)]
    all_gather x1 -> x0, waiting for transfers between devices: 78.1 us -> none  [shards(): weights = lax.all_gather(attn_weight, DP, axis=0, tiled=True)]
    dot_general x11 -> x0, matrix products: 35.5 us -> none  [the longest x3 8.43 us: attend(): jnp.einsum('bhqk,bkhd->bqhd', probs, parts[:, :, 2], preferred_element_ty...]
    all_to_all x3 -> x0, starting transfers between devices: 24.9 us -> none  [copy_for_each(): lax.all_to_all(jnp.broadcast_to(value[None], (count, *value.shape)), axis...]
    all_to_all x3 -> x0, waiting for transfers between devices: 24.4 us -> none  [copy_for_each(): lax.all_to_all(jnp.broadcast_to(value[None], (count, *value.shape)), axis...]
    reduce_sum x11 -> x0, other arithmetic: 14.9 us -> none  [the longest x1 5.51 us: attend(): highest = jnp.max(logits, axis=-1, keepdims=True)]
    convert_element_type x3 -> x0, local copies, waits for them, and re-layouts: 13.5 us -> none  [the longest x1 7.17 us: shards(): qkv = qkv.astype(jnp.bfloat16).reshape(q_local * c_local, seq, 3 * width)]
  transfers between devices with their start and end apart: 6 -> 0, of which waited for: 6 -> 0; matrix products, arithmetic and copies ran while one was open for 4% -> 0% of each run, Pallas kernels for 0% -> 0%
where the time goes in v1:
time: 110 us
  Pallas kernels  104 us (95%)
  local copies, waits for them, and re-layouts  4.94 us (4%)
    pallas_call x1, Pallas kernels, shards(): pl.pallas_call(functools.partial(step_kernel, (X, Z, Y, C)), out_shape=(j...  104 us

profile of v1, /device:TPU:1, one launch (start us, length us, event | category | flops | bytes accessed | tf_op | source)
XLA Modules:
  0.0 110.0 jit_solution(6004894764729211925)
XLA Ops:
  0.6 1.3 %broadcast_in_dim.6.gain = f32[1,768]{1,0:T(1,128)} reshape(f32[768]{0:T(1024)} %param.9) | data formatting | bytes 6144 | tf_op jit(solution)/shard_map/broadcast_in_dim | solution.py:439
  1.9 1.3 %broadcast_in_dim.7.sw = f32[1,768]{1,0:T(1,128)} reshape(f32[768]{0:T(1024)} %param.11) | data formatting | bytes 6144 | tf_op jit(solution)/shard_map/broadcast_in_dim | solution.py:439
  3.2 103.8 %shard_map.86 = (f32[24,3072]{1,0:T(8,128)}, f32[8,128]{1,0:T(8,128)}) custom-call(bf16[2,4,128,768]{3,2,1,0:T(8,128)(2,1)} %hid.1, bf16[24,3072]{1,0:T(8,128)(2,1)} %wsh.1, f32[1,768]{1,0:T(1,128)} %broadcast_in_dim.6.gain, f32[12,128,128]{2,1,0:T(8,128)} %bias.1, f32[1,768]{1,0:T(1,128)} %broadcast_in_dim.7.sw, s32[2,4]{1,0:T(2,128)} %lens.1, s32[2,4]{1,0:T(2,128)} %labs.1), custom_call_target="tpu_custom_call" | custom-call | tf_op jit(solution)/shard_map/pallas_call | solution.py:394
  107.0 0.7 slice.3
  107.7 0.6 reduce
  108.3 1.7 %copy.10 = f32[24,3072]{1,0:T(8,128)} copy(f32[24,3072]{1,0:T(8,128)} %get-tuple-element.8) | data formatting | bytes 589824

commit v2 on v1

--- a/solution.py
+++ b/solution.py
@@ -24,9 +24,9 @@
     return lax.broadcasted_iota(jnp.int32, shape, axis)
 
 
-def step_kernel(dims, hid, wsh, gain, bias, sw, lens, labs, upd, loss, norm, norm_t, w, qk, prob, grad, hsum, svec, avec, uvec, dqk,
-                zbuf, exb, r0, a1, a1s, b1, b1s, a2, b2, zs, z3, ob, sq,
-                zsem, xsem, fsem, dsem, esem, r0sem, a1sem, b1sem, a2sem, b2sem, z3sem, obsem, sqsem):
+def step_kernel(dims, hid_in, wsh_in, gain, bias_in, sw, lens, labs, upd, loss, total_out, hid, wsh, bias, norm, norm_t, w, qk, prob, grad,
+                hsum, svec, avec, uvec, dqk, zc, za, exb, r0, a0, b0, a1, a1s, b1, b1s, a2, b2, zs, z3, ob, sq,
+                lsem, zsem, xsem, xfsem, ysem, yfsem, dsem, esem, r0sem, a0sem, b0sem, a1sem, b1sem, a2sem, b2sem, z3sem, obsem, sqsem):
     X, Z, Y, C = dims
     QL, CL, T, D = hid.shape
     H = bias.shape[0]
@@ -35,6 +35,7 @@
     R = wsh.shape[0]
     XR = Z * R
     HR = XR // 2
+    HQ = HR // 2
     ZH = Z // 2
     NC = 4 * D // PARTS // C
     NB = NC // Y
@@ -67,22 +68,23 @@
     def cols(n, width):
         return pl.ds(pl.multiple_of(n, LANES), width)
 
+    loads = [pltpu.make_async_copy(src, dst, lsem.at[i]) for i, (src, dst) in enumerate(((hid_in, hid), (wsh_in, wsh), (bias_in, bias)))]
+    for load in loads:
+        load.start()
+
+    near_x = [1] if X == 2 else [1, X - 1]
+    near_y = [1] if Y == 2 else [1, Y - 1]
+    first = [at_z(d) for d in range(1, Z)] + [at_x(d) for d in near_x] + [at_y(d) for d in near_y] + [{"c": other}]
     bar = pltpu.get_barrier_semaphore()
-
-    def greet_dp(i, carry):
-        pl.semaphore_signal(bar, 1, device_id=at_dp(i), device_id_type=MESH)
-        return carry
-
-    lax.fori_loop(1, X * Z, greet_dp, 0)
-    for i in range(1, Y * C):
-        pl.semaphore_signal(bar, 1, device_id=at_cand(i), device_id_type=MESH)
+    for to in first:
+        pl.semaphore_signal(bar, 1, device_id=to, device_id_type=MESH)
 
     def pair_len(p):
         return lens[p // CL, lax.rem(p, CL)]
 
     def normalise(p, carry):
         v = hid[p // CL, lax.rem(p, CL)].astype(F32)
-        n = v * lax.rsqrt(jnp.mean(v * v, axis=1, keepdims=True) + EPS) * gain[...]
+        n = v * lax.rsqrt(jnp.mean(v * v, axis=1, keepdims=True) + EPS) * gain_row
         rows = pl.ds(pl.multiple_of(p * T, T), T)
         norm[rows, :] = n.astype(BF16)
         norm_t[:, cols(p * T, T)] = n.T.astype(BF16)
@@ -90,64 +92,136 @@
         hsum[pl.ds(p, 1), :] = jnp.sum(jnp.where(live, v, 0.0), axis=0, keepdims=True)
         return carry
 
+    gain_row, sw_row = gain[...].reshape(1, D), sw[...].reshape(1, D)
+    loads[0].wait()
     lax.fori_loop(0, NP, normalise, 0)
-    pl.semaphore_wait(bar, X * Z - 1 + Y * C - 1)
-
-    def part_cols(g, core):
-        return cols((2 * g + core) * D, D)
-
-    zcopies = {}
-    for g in (0, 1):
-        for d in range(1, Z):
-            zcopies[g, d] = put(wsh.at[:, part_cols(g, c)], zbuf.at[g, z], zsem.at[g, d], at_z(d))
-        zbuf[g, z] = wsh[:, part_cols(g, c)]
+    loads[1].wait()
+    pl.semaphore_wait(bar, len(first))
+
+    AW = D - Y * LANES
+    wide = {"c": LANES, "a": AW}
+
+    def wcols(g, core, kind, yy=0):
+        base = (2 * g + core) * D
+        return cols(base + yy * LANES, LANES) if kind == "c" else cols(base + Y * LANES, AW)
+
+    def yrel(e):
+        return lax.rem(y + e + Y, Y)
 
     def rows_of(d, lo=0, n=XR):
         return pl.ds(pl.multiple_of(lax.rem(x + d + X, X) * XR + lo, HR), n)
 
-    near = [1] if X == 2 else [1, X - 1]
-    xcopies, fcopies, dcopies = {}, {}, {}
-
-    def gather_first(g):
+    zcopies, xcopies, xfcopies, ycopies, yfcopies, dcopies = {}, {}, {}, {}, {}, {}
+    zbuf = {"c": zc, "a": za}
+    kinds = ("c", "a")
+
+    def z_start(g):
+        for i, kind in enumerate(kinds):
+            here = wcols(g, c, kind, y)
+            for d in range(1, Z):
+                zcopies[g, kind, d] = put(wsh.at[:, here], zbuf[kind].at[g, z], zsem.at[g, i, d], at_z(d))
+            zbuf[kind][g, z] = wsh[:, here]
+
+    def x_start(g, kind):
+        i = kinds.index(kind)
         for d in range(1, Z):
-            zcopies[g, d].wait_recv()
-        for k in range(0, D, 256):
-            blk = zbuf[g, :, :, k : k + 256].astype(F32).reshape(XR, 256).astype(BF16)
-            w[rows_of(0), cols((2 * g + c) * D + k, 256)] = blk
-        own = w.at[rows_of(0), part_cols(g, c)]
-        for d in near:
-            xcopies[g, d] = put(own, own, xsem.at[g, d], at_x(d))
-        dcopies[g, 0] = put(own, own, dsem.at[g, 0], {"c": other})
-
-    def gather_second(g):
-        for d in near:
-            xcopies[g, d].wait_recv()
+            zcopies[g, kind, d].wait_recv()
+        here = wcols(g, c, kind, y)
+        w[rows_of(0), here] = zbuf[kind][g].astype(F32).reshape(XR, wide[kind]).astype(BF16)
+        own = w.at[rows_of(0), here]
+        for j, d in enumerate(near_x):
+            xcopies[g, kind, d] = put(own, own, xsem.at[g, i, j], at_x(d))
+
+    def x_forward(g, kind):
+        i = kinds.index(kind)
+        for j, d in enumerate(near_x):
+            xcopies[g, kind, d].wait_recv()
             if X == 4:
-                half = w.at[rows_of(-d, 0 if d == 1 else HR, HR), part_cols(g, c)]
-                fcopies[g, d] = put(half, half, fsem.at[g, d], at_x(d))
-            blk = w.at[rows_of(-d), part_cols(g, c)]
-            dcopies[g, d] = put(blk, blk, dsem.at[g, d], {"c": other})
-
-    def gather_third(g):
+                half = w.at[rows_of(-d, 0 if d == 1 else HR, HR), wcols(g, c, kind, y)]
+                xfcopies[g, kind, d] = put(half, half, xfsem.at[g, i, j], at_x(d))
+
+    def x_last(g, kind):
         if X == 4:
-            for d in near:
-                fcopies[g, d].wait_recv()
-            blk = w.at[rows_of(2), part_cols(g, c)]
-            dcopies[g, 2] = put(blk, blk, dsem.at[g, 2], {"c": other})
-
-    def gather_last(g):
-        for d in range(X):
-            dcopies[g, d].wait_recv()
-
-    gather_first(0)
-    gather_second(0)
-    gather_third(0)
-    gather_first(1)
-    gather_last(0)
+            for d in near_x:
+                xfcopies[g, kind, d].wait_recv()
+
+    def y_start(g, d):
+        blk = w.at[rows_of(d), wcols(g, c, "c", y)]
+        for j, e in enumerate(near_y):
+            ycopies[g, d, e] = put(blk, blk, ysem.at[g, d, j], at_y(e))
+
+    def y_forward(g, d):
+        for j, e in enumerate(near_y):
+            ycopies[g, d, e].wait_recv()
+            if Y == 4:
+                half = w.at[rows_of(d, 0 if e == 1 else HR, HR), wcols(g, c, "c", yrel(-e))]
+                yfcopies[g, d, e] = put(half, half, yfsem.at[g, d, j], at_y(e))
+
+    def y_last(g):
+        if Y == 4:
+            for d in range(X):
+                for e in near_y:
+                    yfcopies[g, d, e].wait_recv()
+
+    def hand_over(g, k, kind, yy=0):
+        blk = w.at[:, wcols(g, c, kind, yy)]
+        dcopies[g, k] = put(blk, blk, dsem.at[g, k], {"c": other})
+
+    def hand_near(g):
+        for e in near_y:
+            hand_over(g, 1 + e, "c", yrel(e))
+
+    def hand_last(g):
+        y_last(g)
+        if Y == 4:
+            hand_over(g, 3, "c", yrel(2))
+
+    def taken(g):
+        for key, copy in dcopies.items():
+            if key[0] == g:
+                copy.wait_recv()
+
+    z_start(0)
+    z_start(1)
+    x_start(0, "c")
+    y_start(0, 0)
+    x_start(0, "a")
+    x_forward(0, "c")
+    for d in near_x:
+        y_start(0, d)
+    y_forward(0, 0)
+    x_forward(0, "a")
+    x_last(0, "c")
+    if X == 4:
+        y_start(0, 2)
+    hand_over(0, 1, "c", y)
+    for d in near_x:
+        y_forward(0, d)
+    x_last(0, "a")
+    hand_over(0, 0, "a")
+    x_start(1, "c")
+    x_start(1, "a")
+    if X == 4:
+        y_forward(0, 2)
+    hand_near(0)
+    y_start(1, 0)
+    hand_last(0)
+    x_forward(1, "c")
+    for d in near_x:
+        y_start(1, d)
+    x_forward(1, "a")
+    taken(0)
 
     for n in range(0, 2 * D, 256):
         qk[:, n : n + 256] = dot(norm[...], w[:, n : n + 256]).astype(BF16)
-    gather_second(1)
+    loads[2].wait()
+    y_forward(1, 0)
+    x_last(1, "c")
+    if X == 4:
+        y_start(1, 2)
+    hand_over(1, 1, "c", y)
+    x_last(1, "a")
+    hand_over(1, 0, "a")
 
     half_lane = iota((1, LANES), 1) < LANES // 2
     ones = [jnp.where(half_lane, 1.0, 0.0).astype(BF16), jnp.where(half_lane, 0.0, 1.0).astype(BF16)]
@@ -177,9 +251,13 @@
         avec[pl.ds(pl.multiple_of(p * 16, 16), 16), :] = a.astype(BF16)
         return carry
 
-    lax.fori_loop(0, NP, attend, 0)
-    gather_third(1)
-    gather_last(1)
+    lax.fori_loop(0, NP // 2, attend, 0)
+    for d in range(1, X):
+        y_forward(1, d)
+    hand_near(1)
+    lax.fori_loop(NP // 2, NP, attend, 0)
+    hand_last(1)
+    taken(1)
 
     wv = w.at[:, 2 * D : 3 * D]
     wo = w.at[:, 3 * D : 4 * D]
@@ -196,7 +274,7 @@
     csum = jnp.sum(jnp.where(head_of[None], zv, 0.0), axis=1)
     pooled = hsum[...] * inv_len + dot((csum * inv_len).astype(BF16), wo[...])
     factor = lax.rsqrt(jnp.mean(pooled * pooled, axis=1, keepdims=True) + EPS)
-    score = jnp.sum(pooled * factor * sw[...], axis=1, keepdims=True)
+    score = jnp.sum(pooled * factor * sw_row, axis=1, keepdims=True)
 
     exb[cand, 0] = jnp.broadcast_to(score, (NP, LANES))
     exb[cand, 1] = jnp.broadcast_to(target, (NP, LANES))
@@ -216,11 +294,13 @@
     expsum = per_query(jnp.sum(jnp.exp(scores - highest[None]), axis=0), jnp.sum, 0.0)
     target_sum = per_query(jnp.sum(targets, axis=0), jnp.sum, 0.0)
     target_dot = per_query(jnp.sum(targets * scores, axis=0), jnp.sum, 0.0)
-    loss[...] = highest + jnp.log(expsum) - target_dot / target_sum
+    losses = highest + jnp.log(expsum) - target_dot / target_sum
+    for k in range(QL):
+        loss[k] = jnp.max(losses[k * CL : k * CL + 1])
     sgrad = (jnp.exp(score - highest) / expsum - target / target_sum)[:, :1]
 
-    along = jnp.sum(pooled * sw[...], axis=1, keepdims=True) * (1.0 / D)
-    pooled_grad = sgrad * (factor * sw[...] - pooled * (factor * factor * factor * along))
+    along = jnp.sum(pooled * sw_row, axis=1, keepdims=True) * (1.0 / D)
+    pooled_grad = sgrad * (factor * sw_row - pooled * (factor * factor * factor * along))
     g = (pooled_grad * inv_len).astype(BF16)
     cg = dot(g, wo[...], 1, 1)
     cexp = jnp.where(head_of[None], cg[:, None, :], 0.0).reshape(NP * 16, D).astype(BF16)
@@ -237,7 +317,7 @@
     for n in range(0, D, 256):
         keep(D + n, dot(avec[...], cexp[:, n : n + 256], 0, 0))
 
-    r0c, a1c, b1c, a2c, b2c, z3c, obc = {}, {}, {}, {}, {}, {}, {}
+    a0c, b0c, r0c, a1c, b1c, a2c, b2c, z3c, obc = {}, {}, {}, {}, {}, {}, {}, {}, {}
 
     def mine(t):
         return cols((t * C + c) * NC, NC)
@@ -248,22 +328,41 @@
     def reduce_1(t):
         r0c[t].wait_recv()
         r0[t] = (r0[t].astype(F32) + grad[:, :, mine(t)].astype(F32)).astype(BF16)
-        for d in range(1, X):
-            a1c[t, d] = put(r0.at[t, lax.rem(x + d, X), :HR, :], a1.at[t, d - 1], a1sem.at[t, d], at_x(d))
-        for d in range(1, Y):
-            to = cols(lax.rem(y + d, Y) * NB, NB)
-            b1c[t, d] = put(r0.at[t, :, HR:, to], b1.at[t, d - 1], b1sem.at[t, d], at_y(d))
+        if X == 4:
+            far = lax.rem(x + 2, X)
+            for j, d in enumerate(near_x):
+                a0c[t, j] = put(r0.at[t, far, j * HQ : (j + 1) * HQ, :], a0.at[t, j], a0sem.at[t, j], at_x(d))
+        if Y == 4:
+            far = cols(yrel(2) * NB, NB)
+            for j, e in enumerate(near_y):
+                b0c[t, j] = put(r0.at[t, :, HR + j * HQ : HR + (j + 1) * HQ, far], b0.at[t, j], b0sem.at[t, j], at_y(e))
+
+    def reduce_1b(t):
+        for j, d in enumerate(near_x):
+            ahead = lax.rem(x + d, X)
+            if X == 4:
+                a0c[t, j].wait_recv()
+                part = pl.ds(j * HQ, HQ)
+                r0[t, ahead, part, :] = (r0[t, ahead, part, :].astype(F32) + a0[t, j].astype(F32)).astype(BF16)
+            a1c[t, j] = put(r0.at[t, ahead, :HR, :], a1.at[t, j], a1sem.at[t, j], at_x(d))
+        for j, e in enumerate(near_y):
+            ahead = cols(yrel(e) * NB, NB)
+            if Y == 4:
+                b0c[t, j].wait_recv()
+                part = pl.ds(HR + j * HQ, HQ)
+                r0[t, :, part, ahead] = (r0[t, :, part, ahead].astype(F32) + b0[t, j].astype(F32)).astype(BF16)
+            b1c[t, j] = put(r0.at[t, :, HR:, ahead], b1.at[t, j], b1sem.at[t, j], at_y(e))
 
     def reduce_2(t):
         total = r0[t, x, :HR, :].astype(F32)
-        for d in range(1, X):
-            a1c[t, d].wait_recv()
-            total += a1[t, d - 1].astype(F32)
+        for j in range(len(near_x)):
+            a1c[t, j].wait_recv()
+            total += a1[t, j].astype(F32)
         a1s[t] = total.astype(BF16)
         total = r0[t, :, HR:, cols(y * NB, NB)].astype(F32)
-        for d in range(1, Y):
-            b1c[t, d].wait_recv()
-            total += b1[t, d - 1].astype(F32)
+        for j in range(len(near_y)):
+            b1c[t, j].wait_recv()
+            total += b1[t, j].astype(F32)
         b1s[t] = total.astype(BF16)
         for d in range(1, Y):
             a2c[t, d] = put(a1s.at[t, :, cols(lax.rem(y + d, Y) * NB, NB)], a2.at[t, d - 1], a2sem.at[t, d], at_y(d))
@@ -316,13 +415,16 @@
     reduce_0(1)
     reduce_1(0)
     lax.fori_loop(2, 4, backward, 0)
+    reduce_1b(0)
     reduce_1(1)
-    reduce_2(0)
     lax.fori_loop(4, HP, backward, 0)
     reduce_0(2)
+    reduce_2(0)
+    reduce_1b(1)
+    reduce_1(2)
+    reduce_3(0)
     reduce_2(1)
-    reduce_3(0)
-    reduce_1(2)
+    reduce_1b(2)
     reduce_3(1)
     reduce_4(0)
     reduce_2(2)
@@ -356,10 +458,6 @@
         return carry
 
     lax.fori_loop(1, X * Z, sq_start, 0)
-    lax.fori_loop(1, X * Z, sq_wait, 0)
-    everything = jnp.sum(sq[...], axis=0)
-    everything = jnp.sum(jnp.sum(everything, axis=1, keepdims=True), axis=0, keepdims=True)
-    scale = 1.0 / (jnp.sqrt(everything * (1.0 / (4.0 * D * D))) + EPS)
     for t in range(PARTS):
         for k in range(Y * C):
             for m in range(NB // LANES):
@@ -370,7 +468,9 @@
                     n = 2 * D + (b - HP) * LANES
                 else:
                     n = (b - 2 * HP) % 2 * D + (b - 2 * HP) // 2 * LANES
-                upd[:, n : n + LANES] = ob[t, k, :, m * LANES : (m + 1) * LANES].astype(F32) * scale
+                upd[:, n : n + LANES] = ob[t, k, :, m * LANES : (m + 1) * LANES]
+    lax.fori_loop(1, X * Z, sq_wait, 0)
+    total_out[0] = jnp.sum(sq[...])
     for copy in started:
         copy.wait_send()
 
@@ -388,15 +488,23 @@
         R = attn_weight.shape[0]
         NP, XR, NC = QL * CL, Z * R, 4 * D // PARTS // C
         HR, NB = XR // 2, NC // Y
+        hbm = pl.BlockSpec(memory_space=pl.ANY)
         vmem, smem = pl.BlockSpec(memory_space=pltpu.VMEM), pl.BlockSpec(memory_space=pltpu.SMEM)
         dma = pltpu.SemaphoreType.DMA
         V = pltpu.VMEM
-        update, loss = pl.pallas_call(
+        summed, loss, squares = pl.pallas_call(
             functools.partial(step_kernel, (X, Z, Y, C)),
-            out_shape=(jax.ShapeDtypeStruct((R, 4 * D), F32), jax.ShapeDtypeStruct((NP, LANES), F32)),
-            in_specs=[vmem] * 5 + [smem] * 2,
-            out_specs=(vmem, vmem),
+            out_shape=(
+                jax.ShapeDtypeStruct((R, 4 * D), BF16),
+                jax.ShapeDtypeStruct((QL,), F32),
+                jax.ShapeDtypeStruct((1,), F32),
+            ),
+            in_specs=[hbm, hbm, vmem, hbm, vmem, smem, smem],
+            out_specs=(vmem, smem, smem),
             scratch_shapes=[
+                V(hidden.shape, BF16),
+                V(attn_weight.shape, BF16),
+                V(pos_bias.shape, F32),
                 V((NP * T, D), BF16),
                 V((D, NP * T), BF16),
                 V((D, 4 * D), BF16),
@@ -408,12 +516,15 @@
                 V((NP * 16, D), BF16),
                 V((NP, 16, T), F32),
                 V((NP * T, 2 * LANES), BF16),
-                V((2, Z, R, D), BF16),
+                V((2, Z, R, LANES), BF16),
+                V((2, Z, R, D - Y * LANES), BF16),
                 V((Y * C, 2, NP, LANES), F32),
                 V((PARTS, X, XR, NC), BF16),
-                V((PARTS, X - 1, HR, NC), BF16),
+                V((PARTS, 2, HR // 2, NC), BF16),
+                V((PARTS, 2, X, HR // 2, NB), BF16),
+                V((PARTS, 2, HR, NC), BF16),
                 V((PARTS, HR, NC), BF16),
-                V((PARTS, Y - 1, X, HR, NB), BF16),
+                V((PARTS, 2, X, HR, NB), BF16),
                 V((PARTS, X, HR, NB), BF16),
                 V((PARTS, Y - 1, HR, NB), BF16),
                 V((PARTS, X - 1, HR, NB), BF16),
@@ -421,14 +532,19 @@
                 V((PARTS, Z - 1, R, NB), BF16),
                 V((PARTS, Y * C, R, NB), BF16),
                 V((X * Z, 8, LANES), F32),
-                dma((2, Z, 2)),
-                dma((2, X, 2)),
-                dma((2, X, 2)),
-                dma((2, X, 2)),
+                dma((3,)),
+                dma((2, 2, Z, 2)),
+                dma((2, 2, 2, 2)),
+                dma((2, 2, 2, 2)),
+                dma((2, X, 2, 2)),
+                dma((2, X, 2, 2)),
+                dma((2, 1 + Y, 2)),
                 dma((Y * C, 2)),
                 dma((PARTS, 2)),
-                dma((PARTS, X, 2)),
-                dma((PARTS, Y, 2)),
+                dma((PARTS, 2, 2)),
+                dma((PARTS, 2, 2)),
+                dma((PARTS, 2, 2)),
+                dma((PARTS, 2, 2)),
                 dma((PARTS, Y, 2)),
                 dma((PARTS, X, 2)),
                 dma((PARTS, Z, 2)),
@@ -436,8 +552,9 @@
                 dma((2, X * Z)),
             ],
             compiler_params=pltpu.CompilerParams(collective_id=0, has_side_effects=True, vmem_limit_bytes=60 * 2**20),
-        )(hidden, attn_weight, norm_gain[None], pos_bias, score_weight[None], pair_lengths, labels)
-        return update, loss[::CL, 0]
+        )(hidden, attn_weight, norm_gain, pos_bias, score_weight, pair_lengths, labels)
+        scale = 1.0 / (jnp.sqrt(squares[0] / (4.0 * D * D)) + EPS)
+        return summed.astype(F32) * scale, loss
 
     placed = (P(dp, cand, None, None), P(dp, None), P(), P(), P(), P(dp, cand), P(dp, cand))
     return jax.shard_map(shards, mesh=split, in_specs=placed, out_specs=(P(dp, None), P(dp)), check_vma=False)

time: 110 us -> 102 us (0.927)
  Pallas kernels: 104 us -> 97.3 us
  local copies, waits for them, and re-layouts: 4.94 us -> 1.16 us
    pallas_call x1, Pallas kernels: 104 us -> 97.3 us  [shards(): pl.pallas_call(functools.partial(step_kernel, (X, Z, Y, C)), out_shape=(j...]
    broadcast_in_dim x2 -> x0, local copies, waits for them, and re-layouts: 2.55 us -> none  [the longest x1 1.28 us: shards(): score_weight[None]]
    mul x0 -> x1, other arithmetic: none -> 1.65 us  [shards(): return (summed.astype(F32) * scale, loss)]
where the time goes in v2:
time: 102 us
  Pallas kernels  97.3 us (95%)
  other arithmetic  1.65 us (2%)
  between operations  1.35 us (1%)
  local copies, waits for them, and re-layouts  1.16 us (1%)
    pallas_call x1, Pallas kernels, shards(): pl.pallas_call(functools.partial(step_kernel, (X, Z, Y, C)), out_shape=(j...  97.3 us

profile of v2, /device:TPU:1, one launch (start us, length us, event | category | flops | bytes accessed | tf_op | source)
XLA Modules:
  0.0 101.5 jit_solution(4172496465502127882)
XLA Ops:
  0.6 97.3 %shard_map.86 = (bf16[24,3072]{1,0:T(8,128)(2,1)}, f32[2]{0:T(128)}, f32[1]{0:T(128)}) custom-call(bf16[2,4,128,768]{3,2,1,0:T(8,128)(2,1)} %hid_in.1, bf16[24,3072]{1,0:T(8,128)(2,1)} %wsh_in.1, f32[768]{0:T(1024)} %gain.1, f32[12,128,128]{2,1,0:T(8,128)} %bias_in.1, f32[768]{0:T(1024)} %sw.1, s32[2,4]{1,0:T(2,128)} %lens.1, s32[2,4]{1,0:T(2,128)} %labs.1), custom_call_target="tpu_custom_call" | custom-call | tf_op jit(solution)/shard_map/pallas_call | solution.py:495
  98.7 1.6 %convert_multiply_fusion = f32[24,3072]{1,0:T(8,128)} fusion(bf16[24,3072]{1,0:T(8,128)(2,1)} %get-tuple-element.5, f32[]{:T(128)} %bitcast), kind=kLoop, calls=%fused_computation | loop fusion | flops 147456 | bytes 442372 | tf_op jit(solution)/shard_map/mul | solution.py:557
  100.3 1.2 %copy.10 = f32[2]{0:T(128)} copy(f32[2]{0:T(128)} %get-tuple-element.11) | data formatting | bytes 16

commit v3 on v2

--- a/solution.py
+++ b/solution.py
@@ -25,12 +25,15 @@
 
 
 def step_kernel(dims, hid_in, wsh_in, gain, bias_in, sw, lens, labs, upd, loss, total_out, hid, wsh, bias, norm, norm_t, w, qk, prob, grad,
-                hsum, svec, avec, uvec, dqk, zc, za, exb, r0, a0, b0, a1, a1s, b1, b1s, a2, b2, zs, z3, ob, sq,
-                lsem, zsem, xsem, xfsem, ysem, yfsem, dsem, esem, r0sem, a0sem, b0sem, a1sem, b1sem, a2sem, b2sem, z3sem, obsem, sqsem):
+                hsum, svec, avec, uvec, dqk, dsend, mixed, zc, za, exb, a0, b0, a1, a1s, b1, b1s, a2, b2, zs, z3, ob, sqz, sq,
+                lsem, zsem, xsem, xfsem, ysem, yfsem, dsem, psem, qsem, esem, a0sem, b0sem, a1sem, b1sem, a2sem, b2sem, z3sem, obsem,
+                sqzsem, sqsem):
     X, Z, Y, C = dims
     QL, CL, T, D = hid.shape
     H = bias.shape[0]
     HP = H // 2
+    HC = HP // C
+    DC = D // C
     NP = QL * CL
     R = wsh.shape[0]
     XR = Z * R
@@ -56,9 +59,6 @@
     def at_cand(i):
         return {"y": lax.rem(y + i // C, Y), "c": lax.rem(c + i % C, C)}
 
-    def at_dp(i):
-        return {"x": lax.rem(x + i // Z, X), "z": lax.rem(z + lax.rem(i, Z), Z)}
-
     def put(src, dst, sems, to):
         copy = pltpu.make_async_remote_copy(src, dst, sems.at[0], sems.at[1], device_id=to, device_id_type=MESH)
         copy.start()
@@ -87,7 +87,7 @@
         n = v * lax.rsqrt(jnp.mean(v * v, axis=1, keepdims=True) + EPS) * gain_row
         rows = pl.ds(pl.multiple_of(p * T, T), T)
         norm[rows, :] = n.astype(BF16)
-        norm_t[:, cols(p * T, T)] = n.T.astype(BF16)
+        norm_t[c, :, cols(p * T, T)] = n.T.astype(BF16)
         live = iota((T, 1), 0) < pair_len(p)
         hsum[pl.ds(p, 1), :] = jnp.sum(jnp.where(live, v, 0.0), axis=0, keepdims=True)
         return carry
@@ -97,6 +97,11 @@
     lax.fori_loop(0, NP, normalise, 0)
     loads[1].wait()
     pl.semaphore_wait(bar, len(first))
+
+    def swap(ref, sem):
+        return put(ref, ref, sem, {"c": other})
+
+    norm_copy = swap(norm_t.at[c], psem.at[0])
 
     AW = D - Y * LANES
     wide = {"c": LANES, "a": AW}
@@ -176,10 +181,53 @@
         if Y == 4:
             hand_over(g, 3, "c", yrel(2))
 
-    def taken(g):
-        for key, copy in dcopies.items():
-            if key[0] == g:
-                copy.wait_recv()
+    def taken(g, keys):
+        for k in keys:
+            dcopies[g, k].wait_recv()
+
+    def attend_a():
+        taken(0, [0])
+        lax.fori_loop(Y, HP, attend, 0)
+
+    def attend_own():
+        taken(0, [1])
+        attend(y, 0)
+
+    def attend_near():
+        taken(0, [1 + e for e in near_y])
+        lax.fori_loop(0, len(near_y), lambda i, carry: attend(lax.rem(y + 1 + i * (Y - 2), Y), carry), 0)
+
+    def attend_far():
+        if Y == 4:
+            taken(0, [3])
+            attend(yrel(2), 0)
+
+    half_lane = iota((1, LANES), 1) < LANES // 2
+    ones = [jnp.where(half_lane, 1.0, 0.0).astype(BF16), jnp.where(half_lane, 0.0, 1.0).astype(BF16)]
+
+    def both(v):
+        return jnp.concatenate([v * ones[0], v * ones[1]], axis=0)
+
+    svec[...] = jnp.zeros_like(svec)
+
+    def attend(h, carry):
+        wqk = jnp.concatenate([w[:, cols(h * LANES, LANES)], w[:, cols(D + h * LANES, LANES)]], axis=1)
+        qk[h] = dot(norm[...], wqk).astype(BF16)
+        for p in range(NP):
+            n_live = lens[p // CL, p % CL]
+            live_key = iota((1, T), 1) < n_live
+            live_row = iota((T, 1), 0) < n_live
+            q2 = qk[h, p * T : (p + 1) * T, :LANES]
+            k2 = qk[h, p * T : (p + 1) * T, LANES:]
+            s = dot(both(q2), k2, 1, 1) + bias[pl.ds(2 * h, 2)].reshape(2 * T, T)
+            s = jnp.where(live_key, s, NEG)
+            e = jnp.exp(s - jnp.max(s, axis=1, keepdims=True))
+            pr = (e * (1.0 / jnp.sum(e, axis=1, keepdims=True))).astype(BF16)
+            prob[p, h] = pr
+            for k in (0, 1):
+                pk = jnp.where(live_row, pr[k * T : (k + 1) * T].astype(F32), 0.0)
+                svec[p, pl.ds(2 * h + k, 1), :] = jnp.sum(pk, axis=0, keepdims=True)
+        return carry
 
     z_start(0)
     z_start(1)
@@ -189,8 +237,11 @@
     x_forward(0, "c")
     for d in near_x:
         y_start(0, d)
+    x_start(1, "c")
+    y_start(1, 0)
     y_forward(0, 0)
     x_forward(0, "a")
+    x_start(1, "a")
     x_last(0, "c")
     if X == 4:
         y_start(0, 2)
@@ -199,65 +250,36 @@
         y_forward(0, d)
     x_last(0, "a")
     hand_over(0, 0, "a")
-    x_start(1, "c")
-    x_start(1, "a")
+    x_forward(1, "c")
+    for d in near_x:
+        y_start(1, d)
     if X == 4:
         y_forward(0, 2)
     hand_near(0)
-    y_start(1, 0)
-    hand_last(0)
-    x_forward(1, "c")
-    for d in near_x:
-        y_start(1, d)
     x_forward(1, "a")
-    taken(0)
-
-    for n in range(0, 2 * D, 256):
-        qk[:, n : n + 256] = dot(norm[...], w[:, n : n + 256]).astype(BF16)
+    y_forward(1, 0)
     loads[2].wait()
-    y_forward(1, 0)
+    attend_a()
     x_last(1, "c")
     if X == 4:
         y_start(1, 2)
+    hand_last(0)
     hand_over(1, 1, "c", y)
     x_last(1, "a")
     hand_over(1, 0, "a")
-
-    half_lane = iota((1, LANES), 1) < LANES // 2
-    ones = [jnp.where(half_lane, 1.0, 0.0).astype(BF16), jnp.where(half_lane, 0.0, 1.0).astype(BF16)]
-
-    def both(v):
-        return jnp.concatenate([v * ones[0], v * ones[1]], axis=0)
-
-    svec[...] = jnp.zeros_like(svec)
-
-    def attend(p, carry):
-        rows = pl.ds(pl.multiple_of(p * T, T), T)
-        n_live = pair_len(p)
-        live_key = iota((1, T), 1) < n_live
-        live_row = iota((T, 1), 0) < n_live
-        for h in range(HP):
-            q2 = qk[rows, h * LANES : (h + 1) * LANES]
-            k2 = qk[rows, D + h * LANES : D + (h + 1) * LANES]
-            s = dot(both(q2), k2, 1, 1) + bias[2 * h : 2 * h + 2].reshape(2 * T, T)
-            s = jnp.where(live_key, s, NEG)
-            e = jnp.exp(s - jnp.max(s, axis=1, keepdims=True))
-            pr = (e * (1.0 / jnp.sum(e, axis=1, keepdims=True))).astype(BF16)
-            prob[p, h] = pr
-            for k in (0, 1):
-                pk = jnp.where(live_row, pr[k * T : (k + 1) * T].astype(F32), 0.0)
-                svec[p, 2 * h + k : 2 * h + k + 1, :] = jnp.sum(pk, axis=0, keepdims=True)
-        a = dot(svec[p].astype(BF16), norm[rows, :])
-        avec[pl.ds(pl.multiple_of(p * 16, 16), 16), :] = a.astype(BF16)
-        return carry
-
-    lax.fori_loop(0, NP // 2, attend, 0)
-    for d in range(1, X):
+    attend_own()
+    for d in near_x:
         y_forward(1, d)
+    attend_near()
+    if X == 4:
+        y_forward(1, 2)
     hand_near(1)
-    lax.fori_loop(NP // 2, NP, attend, 0)
+    attend_far()
     hand_last(1)
-    taken(1)
+    for p in range(NP):
+        avec[c, p * 16 : (p + 1) * 16, :] = dot(svec[p].astype(BF16), norm[p * T : (p + 1) * T, :]).astype(BF16)
+    avec_copy = swap(avec.at[c], psem.at[1])
+    taken(1, [0, 1] + [1 + e for e in near_y] + ([3] if Y == 4 else []))
 
     wv = w.at[:, 2 * D : 3 * D]
     wo = w.at[:, 3 * D : 4 * D]
@@ -270,7 +292,7 @@
     inv_len = 1.0 / length
     target = jnp.exp(target)
 
-    zv = dot(avec[...], wv[...]).reshape(NP, 16, D)
+    zv = dot(avec[c], wv[...]).reshape(NP, 16, D)
     csum = jnp.sum(jnp.where(head_of[None], zv, 0.0), axis=1)
     pooled = hsum[...] * inv_len + dot((csum * inv_len).astype(BF16), wo[...])
     factor = lax.rsqrt(jnp.mean(pooled * pooled, axis=1, keepdims=True) + EPS)
@@ -305,37 +327,44 @@
     cg = dot(g, wo[...], 1, 1)
     cexp = jnp.where(head_of[None], cg[:, None, :], 0.0).reshape(NP * 16, D).astype(BF16)
     tv = dot(cexp, wv[...], 1, 1).astype(BF16)
+    for k, v in enumerate((csum.astype(BF16), g, cg.astype(BF16))):
+        mixed[c, k] = v
+    mixed_copy = swap(mixed.at[c], psem.at[2])
     for p in range(NP):
-        uvec[p] = dot(tv[p * 16 : (p + 1) * 16], norm_t[:, p * T : (p + 1) * T])
+        uvec[p] = dot(tv[p * 16 : (p + 1) * 16], norm_t[c, :, p * T : (p + 1) * T])
 
     def keep(n, value):
         grad[:, :, n : n + value.shape[1]] = value.astype(BF16).reshape(X, XR, value.shape[1])
 
-    csum_b = csum.astype(BF16)
-    for n in range(0, D, 256):
-        keep(n, dot(csum_b, g[:, n : n + 256], 0, 0))
-    for n in range(0, D, 256):
-        keep(D + n, dot(avec[...], cexp[:, n : n + 256], 0, 0))
-
-    a0c, b0c, r0c, a1c, b1c, a2c, b2c, z3c, obc = {}, {}, {}, {}, {}, {}, {}, {}, {}
-
-    def mine(t):
-        return cols((t * C + c) * NC, NC)
-
-    def reduce_0(t):
-        r0c[t] = put(grad.at[:, :, cols((t * C + other) * NC, NC)], r0.at[t], r0sem.at[t], {"c": other})
+    def keep_outer():
+        avec_copy.wait_recv()
+        mixed_copy.wait_recv()
+        mine = cols(c * DC, DC)
+        sums = jnp.concatenate([mixed[k, 0].astype(F32) for k in range(C)], axis=0).astype(BF16)
+        outs = jnp.concatenate([mixed[k, 1, :, mine].astype(F32) for k in range(C)], axis=0).astype(BF16)
+        keep(0, dot(sums, outs, 0, 0))
+        lane_head = (c * DC + iota((16, DC), 1)) // (D // H) == iota((16, DC), 0)
+        total = 0.0
+        for k in range(C):
+            spread = jnp.where(lane_head[None], mixed[k, 2, :, mine].astype(F32)[:, None, :], 0.0).reshape(NP * 16, DC).astype(BF16)
+            total += dot(avec[k], spread, 0, 0)
+        keep(DC, total)
+
+    a0c, b0c, a1c, b1c, a2c, b2c, z3c, obc = {}, {}, {}, {}, {}, {}, {}, {}
+
+    def lanes_of(t, yy=None):
+        return pl.ds(t * NC, NC) if yy is None else cols(t * NC + yy * NB, NB)
 
     def reduce_1(t):
-        r0c[t].wait_recv()
-        r0[t] = (r0[t].astype(F32) + grad[:, :, mine(t)].astype(F32)).astype(BF16)
         if X == 4:
             far = lax.rem(x + 2, X)
             for j, d in enumerate(near_x):
-                a0c[t, j] = put(r0.at[t, far, j * HQ : (j + 1) * HQ, :], a0.at[t, j], a0sem.at[t, j], at_x(d))
+                half = grad.at[far, j * HQ : (j + 1) * HQ, lanes_of(t)]
+                a0c[t, j] = put(half, a0.at[t, j], a0sem.at[t, j], at_x(d))
         if Y == 4:
-            far = cols(yrel(2) * NB, NB)
             for j, e in enumerate(near_y):
-                b0c[t, j] = put(r0.at[t, :, HR + j * HQ : HR + (j + 1) * HQ, far], b0.at[t, j], b0sem.at[t, j], at_y(e))
+                half = grad.at[:, HR + j * HQ : HR + (j + 1) * HQ, lanes_of(t, yrel(2))]
+                b0c[t, j] = put(half, b0.at[t, j], b0sem.at[t, j], at_y(e))
 
     def reduce_1b(t):
         for j, d in enumerate(near_x):
@@ -343,23 +372,23 @@
             if X == 4:
                 a0c[t, j].wait_recv()
                 part = pl.ds(j * HQ, HQ)
-                r0[t, ahead, part, :] = (r0[t, ahead, part, :].astype(F32) + a0[t, j].astype(F32)).astype(BF16)
-            a1c[t, j] = put(r0.at[t, ahead, :HR, :], a1.at[t, j], a1sem.at[t, j], at_x(d))
+                grad[ahead, part, lanes_of(t)] = (grad[ahead, part, lanes_of(t)].astype(F32) + a0[t, j].astype(F32)).astype(BF16)
+            a1c[t, j] = put(grad.at[ahead, :HR, lanes_of(t)], a1.at[t, j], a1sem.at[t, j], at_x(d))
         for j, e in enumerate(near_y):
-            ahead = cols(yrel(e) * NB, NB)
+            ahead = lanes_of(t, yrel(e))
             if Y == 4:
                 b0c[t, j].wait_recv()
                 part = pl.ds(HR + j * HQ, HQ)
-                r0[t, :, part, ahead] = (r0[t, :, part, ahead].astype(F32) + b0[t, j].astype(F32)).astype(BF16)
-            b1c[t, j] = put(r0.at[t, :, HR:, ahead], b1.at[t, j], b1sem.at[t, j], at_y(e))
+                grad[:, part, ahead] = (grad[:, part, ahead].astype(F32) + b0[t, j].astype(F32)).astype(BF16)
+            b1c[t, j] = put(grad.at[:, HR:, ahead], b1.at[t, j], b1sem.at[t, j], at_y(e))
 
     def reduce_2(t):
-        total = r0[t, x, :HR, :].astype(F32)
+        total = grad[x, :HR, lanes_of(t)].astype(F32)
         for j in range(len(near_x)):
             a1c[t, j].wait_recv()
             total += a1[t, j].astype(F32)
         a1s[t] = total.astype(BF16)
-        total = r0[t, :, HR:, cols(y * NB, NB)].astype(F32)
+        total = grad[:, HR:, lanes_of(t, y)].astype(F32)
         for j in range(len(near_y)):
             b1c[t, j].wait_recv()
             total += b1[t, j].astype(F32)
@@ -392,62 +421,86 @@
         for i in range(1, Y * C):
             obc[t, i] = put(ob.at[t, cand], ob.at[t, cand], obsem.at[t, i], at_cand(i))
 
-    def backward(h, carry):
+    def backward(h, out):
         for p in range(NP):
             n_live = lens[p // CL, p % CL]
             live_row = iota((T, 1), 0) < n_live
-            q2 = qk[p * T : (p + 1) * T, cols(h * LANES, LANES)]
-            k2 = qk[p * T : (p + 1) * T, cols(D + h * LANES, LANES)]
+            rows = pl.ds(p * T, T)
             pr = prob[p, h].astype(F32).reshape(2, T, T)
             ds = []
             for k in (0, 1):
                 pu = pr[k] * uvec[p, pl.ds(2 * h + k, 1), :]
                 mean = jnp.sum(pu, axis=1, keepdims=True)
                 ds.append(jnp.where(live_row, pu - pr[k] * mean, 0.0).astype(BF16))
-            dqk[p * T : (p + 1) * T, :LANES] = dot(jnp.concatenate(ds, axis=1), both(k2)).astype(BF16)
-            dqk[p * T : (p + 1) * T, LANES:] = dot(jnp.concatenate(ds, axis=0), both(q2), 0, 0).astype(BF16)
-        dw = dot(norm_t[...], dqk[...]).astype(BF16)
-        grad[:, :, cols(2 * D + h * 2 * LANES, 2 * LANES)] = dw.reshape(X, XR, 2 * LANES)
+            out[rows, :LANES] = dot(jnp.concatenate(ds, axis=1), both(qk[h, rows, LANES:])).astype(BF16)
+            out[rows, LANES:] = dot(jnp.concatenate(ds, axis=0), both(qk[h, rows, :LANES]), 0, 0).astype(BF16)
+
+    def dqk_copy(i):
+        return pltpu.make_async_remote_copy(
+            dsend.at[i], dqk.at[i, c], qsem.at[0, i], qsem.at[1, i], device_id={"c": other}, device_id_type=MESH
+        )
+
+    def for_partner(i, carry):
+        backward(other * HC + i, dsend.at[i])
+        dqk_copy(i).start()
         return carry
 
-    reduce_0(0)
-    lax.fori_loop(0, 2, backward, 0)
-    reduce_0(1)
+    def for_self(i, carry):
+        backward(c * HC + i, dqk.at[i, c])
+        dqk_copy(i).wait()
+        dw = dot(norm_t[0], dqk[i, 0]) + dot(norm_t[1], dqk[i, 1])
+        grad[:, :, cols(2 * DC + i * 2 * LANES, 2 * LANES)] = dw.astype(BF16).reshape(X, XR, 2 * LANES)
+        return carry
+
+    lax.fori_loop(0, HC, for_partner, 0)
+    keep_outer()
+    norm_copy.wait_recv()
     reduce_1(0)
-    lax.fori_loop(2, 4, backward, 0)
+    lax.fori_loop(0, 1, for_self, 0)
+    reduce_1(1)
     reduce_1b(0)
-    reduce_1(1)
-    lax.fori_loop(4, HP, backward, 0)
-    reduce_0(2)
+    lax.fori_loop(1, HC, for_self, 0)
+    reduce_1(2)
     reduce_2(0)
     reduce_1b(1)
-    reduce_1(2)
+    reduce_1b(2)
     reduce_3(0)
     reduce_2(1)
-    reduce_1b(2)
+    reduce_2(2)
     reduce_3(1)
     reduce_4(0)
-    reduce_2(2)
+    reduce_3(2)
     reduce_4(1)
-    reduce_3(2)
     reduce_4(2)
+    squares = jnp.zeros((R, NB), F32)
+    for t in range(PARTS):
+        v = ob[t, cand].astype(F32)
+        squares += v * v
+    squares = jnp.sum(jnp.sum(squares, axis=1, keepdims=True), axis=0, keepdims=True)
+    sqz[z] = jnp.broadcast_to(squares, (8, LANES))
+    zsq = [put(sqz.at[z], sqz.at[z], sqzsem.at[d], at_z(d)) for d in range(1, Z)]
     for copy in obc.values():
         copy.wait_recv()
-
-    me = x * Z + z
-    squares = jnp.zeros((R, NB), F32)
     for t in range(PARTS):
         for k in range(Y * C):
-            v = ob[t, k].astype(F32)
-            squares += v * v
-    tile = squares.reshape(R // 8, 8, NB // LANES, LANES) if NB > LANES else squares.reshape(R // 8, 8, LANES)
-    tile = jnp.sum(tile, axis=(0, 2)) if NB > LANES else jnp.sum(tile, axis=0)
-    sq[me] = tile
+            for m in range(NB // LANES):
+                b, core = (t * NC + (k // C) * NB) // LANES + m, k % C
+                outer = DC // LANES
+                if b < outer:
+                    n = 3 * D + core * DC + b * LANES
+                elif b < 2 * outer:
+                    n = 2 * D + core * DC + (b - outer) * LANES
+                else:
+                    n = (b - 2 * outer) % 2 * D + (core * HC + (b - 2 * outer) // 2) * LANES
+                upd[:, n : n + LANES] = ob[t, k, :, m * LANES : (m + 1) * LANES]
+    for copy in zsq:
+        copy.wait_recv()
+    me = x * Y * C + cand
+    sq[me] = jnp.sum(sqz[...], axis=0)
 
     def sq_copy(i):
-        return pltpu.make_async_remote_copy(
-            sq.at[me], sq.at[me], sqsem.at[0, i], sqsem.at[1, i], device_id=at_dp(i), device_id_type=MESH
-        )
+        to = at_cand(lax.rem(i, Y * C)) | at_x(i // (Y * C))
+        return pltpu.make_async_remote_copy(sq.at[me], sq.at[me], sqsem.at[0, i], sqsem.at[1, i], device_id=to, device_id_type=MESH)
 
     def sq_start(i, carry):
         sq_copy(i).start()
@@ -457,20 +510,9 @@
         sq_copy(i).wait()
         return carry
 
-    lax.fori_loop(1, X * Z, sq_start, 0)
-    for t in range(PARTS):
-        for k in range(Y * C):
-            for m in range(NB // LANES):
-                b = ((t * C + k % C) * NC + (k // C) * NB) // LANES + m
-                if b < HP:
-                    n = 3 * D + b * LANES
-                elif b < 2 * HP:
-                    n = 2 * D + (b - HP) * LANES
-                else:
-                    n = (b - 2 * HP) % 2 * D + (b - 2 * HP) // 2 * LANES
-                upd[:, n : n + LANES] = ob[t, k, :, m * LANES : (m + 1) * LANES]
-    lax.fori_loop(1, X * Z, sq_wait, 0)
-    total_out[0] = jnp.sum(sq[...])
+    lax.fori_loop(1, X * Y * C, sq_start, 0)
+    lax.fori_loop(1, X * Y * C, sq_wait, 0)
+    total_out[0] = jnp.max(jnp.sum(sq[...], axis=0))
     for copy in started:
         copy.wait_send()
 
@@ -506,20 +548,21 @@
                 V(attn_weight.shape, BF16),
                 V(pos_bias.shape, F32),
                 V((NP * T, D), BF16),
-                V((D, NP * T), BF16),
+                V((C, D, NP * T), BF16),
                 V((D, 4 * D), BF16),
-                V((NP * T, 2 * D), BF16),
+                V((H // 2, NP * T, 2 * LANES), BF16),
                 V((NP, H // 2, 2 * T, T), BF16),
-                V((X, XR, 4 * D), BF16),
+                V((X, XR, 4 * D // C), BF16),
                 V((NP, D), F32),
                 V((NP, 16, T), F32),
-                V((NP * 16, D), BF16),
+                V((C, NP * 16, D), BF16),
                 V((NP, 16, T), F32),
-                V((NP * T, 2 * LANES), BF16),
+                V((H // 2 // C, C, NP * T, 2 * LANES), BF16),
+                V((H // 2 // C, NP * T, 2 * LANES), BF16),
+                V((C, 3, NP, D), BF16),
                 V((2, Z, R, LANES), BF16),
                 V((2, Z, R, D - Y * LANES), BF16),
                 V((Y * C, 2, NP, LANES), F32),
-                V((PARTS, X, XR, NC), BF16),
                 V((PARTS, 2, HR // 2, NC), BF16),
                 V((PARTS, 2, X, HR // 2, NB), BF16),
                 V((PARTS, 2, HR, NC), BF16),
@@ -531,7 +574,8 @@
                 V((PARTS, Z, R, NB), BF16),
                 V((PARTS, Z - 1, R, NB), BF16),
                 V((PARTS, Y * C, R, NB), BF16),
-                V((X * Z, 8, LANES), F32),
+                V((Z, 8, LANES), F32),
+                V((X * Y * C, 8, LANES), F32),
                 dma((3,)),
                 dma((2, 2, Z, 2)),
                 dma((2, 2, 2, 2)),
@@ -539,8 +583,9 @@
                 dma((2, X, 2, 2)),
                 dma((2, X, 2, 2)),
                 dma((2, 1 + Y, 2)),
+                dma((3, 2)),
+                dma((2, H // 2 // C)),
                 dma((Y * C, 2)),
-                dma((PARTS, 2)),
                 dma((PARTS, 2, 2)),
                 dma((PARTS, 2, 2)),
                 dma((PARTS, 2, 2)),
@@ -549,7 +594,8 @@
                 dma((PARTS, X, 2)),
                 dma((PARTS, Z, 2)),
                 dma((PARTS, Y * C, 2)),
-                dma((2, X * Z)),
+                dma((Z, 2)),
+                dma((2, X * Y * C)),
             ],
             compiler_params=pltpu.CompilerParams(collective_id=0, has_side_effects=True, vmem_limit_bytes=60 * 2**20),
         )(hidden, attn_weight, norm_gain, pos_bias, score_weight, pair_lengths, labels)

time: 102 us -> 95.2 us (0.933)
  Pallas kernels: 97.3 us -> 90.9 us
    pallas_call x1, Pallas kernels: 97.3 us -> 90.9 us  [shards(): pl.pallas_call(functools.partial(step_kernel, (X, Z, Y, C)), out_shape=(j...]
where the time goes in v3:
time: 95.2 us; the launch traced here: 95 us
  Pallas kernels  90.9 us (95%)
  other arithmetic  1.65 us (2%)
  between operations  1.36 us (1%)
  local copies, waits for them, and re-layouts  1.16 us (1%)
    pallas_call x1, Pallas kernels, shards(): pl.pallas_call(functools.partial(step_kernel, (X, Z, Y, C)), out_shape=(j...  90.9 us

profile of v3, /device:TPU:1, one launch (start us, length us, event | category | flops | bytes accessed | tf_op | source)
XLA Modules:
  0.0 95.0 jit_solution(14188746840655500201)
XLA Ops:
  0.6 90.9 %shard_map.86 = (bf16[24,3072]{1,0:T(8,128)(2,1)}, f32[2]{0:T(128)}, f32[1]{0:T(128)}) custom-call(bf16[2,4,128,768]{3,2,1,0:T(8,128)(2,1)} %hid_in.1, bf16[24,3072]{1,0:T(8,128)(2,1)} %wsh_in.1, f32[768]{0:T(1024)} %gain.1, f32[12,128,128]{2,1,0:T(8,128)} %bias_in.1, f32[768]{0:T(1024)} %sw.1, s32[2,4]{1,0:T(2,128)} %lens.1, s32[2,4]{1,0:T(2,128)} %labs.1), custom_call_target="tpu_custom_call" | custom-call | tf_op jit(solution)/shard_map/pallas_call | solution.py:537
  92.2 1.6 %convert_multiply_fusion = f32[24,3072]{1,0:T(8,128)} fusion(bf16[24,3072]{1,0:T(8,128)(2,1)} %get-tuple-element.5, f32[]{:T(128)} %bitcast), kind=kLoop, calls=%fused_computation | loop fusion | flops 147456 | bytes 442372 | tf_op jit(solution)/shard_map/mul | solution.py:603
  93.9 1.2 %copy.10 = f32[2]{0:T(128)} copy(f32[2]{0:T(128)} %get-tuple-element.11) | data formatting | bytes 16

commit v4 on v3

--- a/solution.py
+++ b/solution.py
@@ -24,8 +24,8 @@
     return lax.broadcasted_iota(jnp.int32, shape, axis)
 
 
-def step_kernel(dims, hid_in, wsh_in, gain, bias_in, sw, lens, labs, upd, loss, total_out, hid, wsh, bias, norm, norm_t, w, qk, prob, grad,
-                hsum, svec, avec, uvec, dqk, dsend, mixed, zc, za, exb, a0, b0, a1, a1s, b1, b1s, a2, b2, zs, z3, ob, sqz, sq,
+def step_kernel(dims, hid_in, wsh_in, gain, bias_in, sw, lens, labs, upd, out_s, hid, wsh, bias, norm, norm_t, w, qk, prob, grad,
+                hsum, svec, avec, uvec, dqk, dsend, mixed, zc, za, zv, exb, a0, b0, a1, a1s, b1, b1s, a2, b2, zs, z3, ob, sqz, sq,
                 lsem, zsem, xsem, xfsem, ysem, yfsem, dsem, psem, qsem, esem, a0sem, b0sem, a1sem, b1sem, a2sem, b2sem, z3sem, obsem,
                 sqzsem, sqsem):
     X, Z, Y, C = dims
@@ -93,22 +93,20 @@
         return carry
 
     gain_row, sw_row = gain[...].reshape(1, D), sw[...].reshape(1, D)
-    loads[0].wait()
-    lax.fori_loop(0, NP, normalise, 0)
     loads[1].wait()
     pl.semaphore_wait(bar, len(first))
 
     def swap(ref, sem):
         return put(ref, ref, sem, {"c": other})
 
-    norm_copy = swap(norm_t.at[c], psem.at[0])
 
     AW = D - Y * LANES
-    wide = {"c": LANES, "a": AW}
+    wide = {"c": LANES, "a": AW, 0: 2 * LANES, 1: 2 * LANES, 2: 2 * LANES}
+    kinds = {0: ("c", "a"), 1: (0, 1, 2)}
 
     def wcols(g, core, kind, yy=0):
         base = (2 * g + core) * D
-        return cols(base + yy * LANES, LANES) if kind == "c" else cols(base + Y * LANES, AW)
+        return cols(base + (yy * LANES if kind == "c" else Y * LANES if kind == "a" else kind * 2 * LANES), wide[kind])
 
     def yrel(e):
         return lax.rem(y + e + Y, Y)
@@ -117,28 +115,27 @@
         return pl.ds(pl.multiple_of(lax.rem(x + d + X, X) * XR + lo, HR), n)
 
     zcopies, xcopies, xfcopies, ycopies, yfcopies, dcopies = {}, {}, {}, {}, {}, {}
-    zbuf = {"c": zc, "a": za}
-    kinds = ("c", "a")
+    zbuf = {"c": zc, "a": za, 0: zv.at[0], 1: zv.at[1], 2: zv.at[2]}
 
     def z_start(g):
-        for i, kind in enumerate(kinds):
+        for i, kind in enumerate(kinds[g]):
             here = wcols(g, c, kind, y)
             for d in range(1, Z):
-                zcopies[g, kind, d] = put(wsh.at[:, here], zbuf[kind].at[g, z], zsem.at[g, i, d], at_z(d))
-            zbuf[kind][g, z] = wsh[:, here]
+                zcopies[g, kind, d] = put(wsh.at[:, here], zbuf[kind].at[z], zsem.at[g, i, d], at_z(d))
+            zbuf[kind][z] = wsh[:, here]
 
     def x_start(g, kind):
-        i = kinds.index(kind)
+        i = kinds[g].index(kind)
         for d in range(1, Z):
             zcopies[g, kind, d].wait_recv()
         here = wcols(g, c, kind, y)
-        w[rows_of(0), here] = zbuf[kind][g].astype(F32).reshape(XR, wide[kind]).astype(BF16)
+        w[rows_of(0), here] = zbuf[kind][...].astype(F32).reshape(XR, wide[kind]).astype(BF16)
         own = w.at[rows_of(0), here]
         for j, d in enumerate(near_x):
             xcopies[g, kind, d] = put(own, own, xsem.at[g, i, j], at_x(d))
 
     def x_forward(g, kind):
-        i = kinds.index(kind)
+        i = kinds[g].index(kind)
         for j, d in enumerate(near_x):
             xcopies[g, kind, d].wait_recv()
             if X == 4:
@@ -231,17 +228,18 @@
 
     z_start(0)
     z_start(1)
+    loads[0].wait()
+    lax.fori_loop(0, NP, normalise, 0)
+    norm_copy = swap(norm_t.at[c], psem.at[0])
     x_start(0, "c")
     y_start(0, 0)
     x_start(0, "a")
     x_forward(0, "c")
     for d in near_x:
         y_start(0, d)
-    x_start(1, "c")
-    y_start(1, 0)
     y_forward(0, 0)
     x_forward(0, "a")
-    x_start(1, "a")
+    x_start(1, 0)
     x_last(0, "c")
     if X == 4:
         y_start(0, 2)
@@ -250,36 +248,27 @@
         y_forward(0, d)
     x_last(0, "a")
     hand_over(0, 0, "a")
-    x_forward(1, "c")
-    for d in near_x:
-        y_start(1, d)
+    x_start(1, 1)
+    x_start(1, 2)
     if X == 4:
         y_forward(0, 2)
     hand_near(0)
-    x_forward(1, "a")
-    y_forward(1, 0)
     loads[2].wait()
     attend_a()
-    x_last(1, "c")
-    if X == 4:
-        y_start(1, 2)
+    x_forward(1, 0)
+    x_forward(1, 1)
+    attend_own()
     hand_last(0)
-    hand_over(1, 1, "c", y)
-    x_last(1, "a")
-    hand_over(1, 0, "a")
-    attend_own()
-    for d in near_x:
-        y_forward(1, d)
+    x_forward(1, 2)
     attend_near()
-    if X == 4:
-        y_forward(1, 2)
-    hand_near(1)
+    for k in kinds[1]:
+        x_last(1, k)
+        hand_over(1, k, k)
     attend_far()
-    hand_last(1)
     for p in range(NP):
         avec[c, p * 16 : (p + 1) * 16, :] = dot(svec[p].astype(BF16), norm[p * T : (p + 1) * T, :]).astype(BF16)
     avec_copy = swap(avec.at[c], psem.at[1])
-    taken(1, [0, 1] + [1 + e for e in near_y] + ([3] if Y == 4 else []))
+    taken(1, kinds[1])
 
     wv = w.at[:, 2 * D : 3 * D]
     wo = w.at[:, 3 * D : 4 * D]
@@ -301,54 +290,68 @@
     exb[cand, 0] = jnp.broadcast_to(score, (NP, LANES))
     exb[cand, 1] = jnp.broadcast_to(target, (NP, LANES))
     ecopies = [put(exb.at[cand], exb.at[cand], esem.at[i], at_cand(i)) for i in range(1, Y * C)]
-    for copy in ecopies:
-        copy.wait_recv()
-    scores, targets = exb[:, 0], exb[:, 1]
-    query = iota((NP, LANES), 0) // CL
-
-    def per_query(v, op, neutral):
-        out = v
-        for k in range(QL):
-            out = jnp.where(query == k, op(jnp.where(query == k, v, neutral), axis=0, keepdims=True), out)
-        return out
-
-    highest = per_query(jnp.max(scores, axis=0), jnp.max, -jnp.inf)
-    expsum = per_query(jnp.sum(jnp.exp(scores - highest[None]), axis=0), jnp.sum, 0.0)
-    target_sum = per_query(jnp.sum(targets, axis=0), jnp.sum, 0.0)
-    target_dot = per_query(jnp.sum(targets * scores, axis=0), jnp.sum, 0.0)
-    losses = highest + jnp.log(expsum) - target_dot / target_sum
-    for k in range(QL):
-        loss[k] = jnp.max(losses[k * CL : k * CL + 1])
-    sgrad = (jnp.exp(score - highest) / expsum - target / target_sum)[:, :1]
 
     along = jnp.sum(pooled * sw_row, axis=1, keepdims=True) * (1.0 / D)
-    pooled_grad = sgrad * (factor * sw_row - pooled * (factor * factor * factor * along))
-    g = (pooled_grad * inv_len).astype(BF16)
-    cg = dot(g, wo[...], 1, 1)
+    unit = (factor * sw_row - pooled * (factor * factor * factor * along)) * inv_len
+    unit_b = unit.astype(BF16)
+    cg = dot(unit_b, wo[...], 1, 1)
+    for k, v in enumerate((csum.astype(BF16), unit_b, cg.astype(BF16))):
+        mixed[c, k] = v
+    mixed_copy = swap(mixed.at[c], psem.at[2])
     cexp = jnp.where(head_of[None], cg[:, None, :], 0.0).reshape(NP * 16, D).astype(BF16)
     tv = dot(cexp, wv[...], 1, 1).astype(BF16)
-    for k, v in enumerate((csum.astype(BF16), g, cg.astype(BF16))):
-        mixed[c, k] = v
-    mixed_copy = swap(mixed.at[c], psem.at[2])
     for p in range(NP):
         uvec[p] = dot(tv[p * 16 : (p + 1) * 16], norm_t[c, :, p * T : (p + 1) * T])
 
+    def listwise():
+        for copy in ecopies:
+            copy.wait_recv()
+        scores, targets = exb[:, 0], exb[:, 1]
+        query = iota((NP, LANES), 0) // CL
+
+        def per_query(v, op, neutral):
+            out = v
+            for k in range(QL):
+                out = jnp.where(query == k, op(jnp.where(query == k, v, neutral), axis=0, keepdims=True), out)
+            return out
+
+        highest = per_query(jnp.max(scores, axis=0), jnp.max, -jnp.inf)
+        expsum = per_query(jnp.sum(jnp.exp(scores - highest[None]), axis=0), jnp.sum, 0.0)
+        target_sum = per_query(jnp.sum(targets, axis=0), jnp.sum, 0.0)
+        target_dot = per_query(jnp.sum(targets * scores, axis=0), jnp.sum, 0.0)
+        losses = highest + jnp.log(expsum) - target_dot / target_sum
+        for k in range(QL):
+            out_s[1 + k] = jnp.max(losses[k * CL : k * CL + 1])
+        grads = []
+        for k in range(C):
+            grads.append((jnp.exp(exb[y * C + k, 0] - highest) / expsum - exb[y * C + k, 1] / target_sum)[:, :1])
+        return grads
+
     def keep(n, value):
         grad[:, :, n : n + value.shape[1]] = value.astype(BF16).reshape(X, XR, value.shape[1])
 
-    def keep_outer():
+    def keep_outer(sgrad):
         avec_copy.wait_recv()
         mixed_copy.wait_recv()
         mine = cols(c * DC, DC)
         sums = jnp.concatenate([mixed[k, 0].astype(F32) for k in range(C)], axis=0).astype(BF16)
-        outs = jnp.concatenate([mixed[k, 1, :, mine].astype(F32) for k in range(C)], axis=0).astype(BF16)
+        outs = jnp.concatenate([mixed[k, 1, :, mine].astype(F32) * sgrad[k] for k in range(C)], axis=0).astype(BF16)
         keep(0, dot(sums, outs, 0, 0))
         lane_head = (c * DC + iota((16, DC), 1)) // (D // H) == iota((16, DC), 0)
         total = 0.0
         for k in range(C):
-            spread = jnp.where(lane_head[None], mixed[k, 2, :, mine].astype(F32)[:, None, :], 0.0).reshape(NP * 16, DC).astype(BF16)
+            rows = mixed[k, 2, :, mine].astype(F32) * sgrad[k]
+            spread = jnp.where(lane_head[None], rows[:, None, :], 0.0).reshape(NP * 16, DC).astype(BF16)
             total += dot(avec[k], spread, 0, 0)
         keep(DC, total)
+
+    def scale_norm(sgrad):
+        norm_copy.wait_recv()
+        norm_copy.wait_send()
+        for k in range(C):
+            for p in range(NP):
+                v = norm_t[k, :, p * T : (p + 1) * T].astype(F32) * sgrad[k][p : p + 1]
+                norm_t[k, :, p * T : (p + 1) * T] = v.astype(BF16)
 
     a0c, b0c, a1c, b1c, a2c, b2c, z3c, obc = {}, {}, {}, {}, {}, {}, {}, {}
 
@@ -447,29 +450,34 @@
 
     def for_self(i, carry):
         backward(c * HC + i, dqk.at[i, c])
+        return carry
+
+    def keep_qk(i, carry):
         dqk_copy(i).wait()
         dw = dot(norm_t[0], dqk[i, 0]) + dot(norm_t[1], dqk[i, 1])
         grad[:, :, cols(2 * DC + i * 2 * LANES, 2 * LANES)] = dw.astype(BF16).reshape(X, XR, 2 * LANES)
         return carry
 
     lax.fori_loop(0, HC, for_partner, 0)
-    keep_outer()
-    norm_copy.wait_recv()
+    lax.fori_loop(0, HC, for_self, 0)
+    sgrad = listwise()
+    keep_outer(sgrad)
     reduce_1(0)
-    lax.fori_loop(0, 1, for_self, 0)
+    scale_norm(sgrad)
+    keep_qk(0, 0)
     reduce_1(1)
+    lax.fori_loop(1, HC, keep_qk, 0)
+    reduce_1(2)
     reduce_1b(0)
-    lax.fori_loop(1, HC, for_self, 0)
-    reduce_1(2)
-    reduce_2(0)
     reduce_1b(1)
     reduce_1b(2)
-    reduce_3(0)
+    reduce_2(0)
     reduce_2(1)
     reduce_2(2)
+    reduce_3(0)
     reduce_3(1)
+    reduce_3(2)
     reduce_4(0)
-    reduce_3(2)
     reduce_4(1)
     reduce_4(2)
     squares = jnp.zeros((R, NB), F32)
@@ -478,7 +486,8 @@
         squares += v * v
     squares = jnp.sum(jnp.sum(squares, axis=1, keepdims=True), axis=0, keepdims=True)
     sqz[z] = jnp.broadcast_to(squares, (8, LANES))
-    zsq = [put(sqz.at[z], sqz.at[z], sqzsem.at[d], at_z(d)) for d in range(1, Z)]
+    zline = sqz.at[z, :1]
+    zsq = [put(zline, zline, sqzsem.at[d], at_z(d)) for d in range(1, Z)]
     for copy in obc.values():
         copy.wait_recv()
     for t in range(PARTS):
@@ -496,25 +505,15 @@
     for copy in zsq:
         copy.wait_recv()
     me = x * Y * C + cand
-    sq[me] = jnp.sum(sqz[...], axis=0)
-
-    def sq_copy(i):
-        to = at_cand(lax.rem(i, Y * C)) | at_x(i // (Y * C))
-        return pltpu.make_async_remote_copy(sq.at[me], sq.at[me], sqsem.at[0, i], sqsem.at[1, i], device_id=to, device_id_type=MESH)
-
-    def sq_start(i, carry):
-        sq_copy(i).start()
-        return carry
-
-    def sq_wait(i, carry):
-        sq_copy(i).wait()
-        return carry
-
-    lax.fori_loop(1, X * Y * C, sq_start, 0)
-    lax.fori_loop(1, X * Y * C, sq_wait, 0)
-    total_out[0] = jnp.max(jnp.sum(sq[...], axis=0))
+    sq[me, :1] = jnp.sum(sqz[:, :1], axis=0)
+    line = sq.at[me, :1]
+    sqs = [put(line, line, sqsem.at[i], at_cand(i % (Y * C)) | at_x(i // (Y * C))) for i in range(1, X * Y * C)]
+    for copy in sqs:
+        copy.wait_recv()
+    out_s[0] = jnp.max(jnp.sum(sq[:, :1], axis=0))
     for copy in started:
-        copy.wait_send()
+        if copy is not norm_copy:
+            copy.wait_send()
 
 
 def solution(mesh):
@@ -534,15 +533,14 @@
         vmem, smem = pl.BlockSpec(memory_space=pltpu.VMEM), pl.BlockSpec(memory_space=pltpu.SMEM)
         dma = pltpu.SemaphoreType.DMA
         V = pltpu.VMEM
-        summed, loss, squares = pl.pallas_call(
+        summed, scalars = pl.pallas_call(
             functools.partial(step_kernel, (X, Z, Y, C)),
             out_shape=(
                 jax.ShapeDtypeStruct((R, 4 * D), BF16),
-                jax.ShapeDtypeStruct((QL,), F32),
-                jax.ShapeDtypeStruct((1,), F32),
+                jax.ShapeDtypeStruct((1 + QL,), F32),
             ),
             in_specs=[hbm, hbm, vmem, hbm, vmem, smem, smem],
-            out_specs=(vmem, smem, smem),
+            out_specs=(vmem, smem),
             scratch_shapes=[
                 V(hidden.shape, BF16),
                 V(attn_weight.shape, BF16),
@@ -560,8 +558,9 @@
                 V((H // 2 // C, C, NP * T, 2 * LANES), BF16),
                 V((H // 2 // C, NP * T, 2 * LANES), BF16),
                 V((C, 3, NP, D), BF16),
-                V((2, Z, R, LANES), BF16),
-                V((2, Z, R, D - Y * LANES), BF16),
+                V((Z, R, LANES), BF16),
+                V((Z, R, D - Y * LANES), BF16),
+                V((3, Z, R, 2 * LANES), BF16),
                 V((Y * C, 2, NP, LANES), F32),
                 V((PARTS, 2, HR // 2, NC), BF16),
                 V((PARTS, 2, X, HR // 2, NB), BF16),
@@ -577,11 +576,11 @@
                 V((Z, 8, LANES), F32),
                 V((X * Y * C, 8, LANES), F32),
                 dma((3,)),
-                dma((2, 2, Z, 2)),
-                dma((2, 2, 2, 2)),
-                dma((2, 2, 2, 2)),
-                dma((2, X, 2, 2)),
-                dma((2, X, 2, 2)),
+                dma((2, 3, Z, 2)),
+                dma((2, 3, 2, 2)),
+                dma((2, 3, 2, 2)),
+                dma((1, X, 2, 2)),
+                dma((1, X, 2, 2)),
                 dma((2, 1 + Y, 2)),
                 dma((3, 2)),
                 dma((2, H // 2 // C)),
@@ -595,12 +594,12 @@
                 dma((PARTS, Z, 2)),
                 dma((PARTS, Y * C, 2)),
                 dma((Z, 2)),
-                dma((2, X * Y * C)),
+                dma((X * Y * C, 2)),
             ],
             compiler_params=pltpu.CompilerParams(collective_id=0, has_side_effects=True, vmem_limit_bytes=60 * 2**20),
         )(hidden, attn_weight, norm_gain, pos_bias, score_weight, pair_lengths, labels)
-        scale = 1.0 / (jnp.sqrt(squares[0] / (4.0 * D * D)) + EPS)
-        return summed.astype(F32) * scale, loss
+        scale = 1.0 / (jnp.sqrt(scalars[0] / (4.0 * D * D)) + EPS)
+        return summed.astype(F32) * scale, scalars[1:]
 
     placed = (P(dp, cand, None, None), P(dp, None), P(), P(), P(), P(dp, cand), P(dp, cand))
     return jax.shard_map(shards, mesh=split, in_specs=placed, out_specs=(P(dp, None), P(dp)), check_vma=False)

time: 95.2 us -> 90.4 us (0.950)
  Pallas kernels: 90.9 us -> 86 us
    pallas_call x1, Pallas kernels: 90.9 us -> 86 us  [shards(): pl.pallas_call(functools.partial(step_kernel, (X, Z, Y, C)), out_shape=(j...]
    slice x0 -> x1, local copies, waits for them, and re-layouts: none -> 1.23 us  [shards(): return (summed.astype(F32) * scale, scalars[1:])]
    unnamed x1 -> x0, local copies, waits for them, and re-layouts: 1.16 us -> none
where the time goes in v4:
time: 90.4 us; the launch traced here: 90.3 us
  Pallas kernels  86 us (95%)
  other arithmetic  1.64 us (2%)
  between operations  1.35 us (1%)
  local copies, waits for them, and re-layouts  1.23 us (1%)
    pallas_call x1, Pallas kernels, shards(): pl.pallas_call(functools.partial(step_kernel, (X, Z, Y, C)), out_shape=(j...  86 us

profile of v4, /device:TPU:1, one launch (start us, length us, event | category | flops | bytes accessed | tf_op | source)
XLA Modules:
  0.0 90.3 jit_solution(11871131674447519273)
XLA Ops:
  0.6 86.0 %shard_map.86 = (bf16[24,3072]{1,0:T(8,128)(2,1)}, f32[3]{0:T(128)}) custom-call(bf16[2,4,128,768]{3,2,1,0:T(8,128)(2,1)} %hid_in.1, bf16[24,3072]{1,0:T(8,128)(2,1)} %wsh_in.1, f32[768]{0:T(1024)} %gain.1, f32[12,128,128]{2,1,0:T(8,128)} %bias_in.1, f32[768]{0:T(1024)} %sw.1, s32[2,4]{1,0:T(2,128)} %lens.1, s32[2,4]{1,0:T(2,128)} %labs.1), custom_call_target="tpu_custom_call" | custom-call | tf_op jit(solution)/shard_map/pallas_call | solution.py:536
  87.4 1.2 %slice.7 = f32[2]{0:T(128)} slice(f32[3]{0:T(128)} %get-tuple-element.5), slice={[1:3]} | slice | bytes 16 | tf_op jit(solution)/shard_map/slice | solution.py:602
  88.6 1.6 %convert_multiply_fusion = f32[24,3072]{1,0:T(8,128)} fusion(bf16[24,3072]{1,0:T(8,128)(2,1)} %get-tuple-element.4, f32[]{:T(128)} %bitcast), kind=kLoop, calls=%fused_computation | loop fusion | flops 147456 | bytes 442372 | tf_op jit(solution)/shard_map/mul | solution.py:602

commit v5 on v4

--- a/solution.py
+++ b/solution.py
@@ -115,7 +115,7 @@
         return pl.ds(pl.multiple_of(lax.rem(x + d + X, X) * XR + lo, HR), n)
 
     zcopies, xcopies, xfcopies, ycopies, yfcopies, dcopies = {}, {}, {}, {}, {}, {}
-    zbuf = {"c": zc, "a": za, 0: zv.at[0], 1: zv.at[1], 2: zv.at[2]}
+    zbuf = {"c": zc, "a": za}
 
     def z_start(g):
         for i, kind in enumerate(kinds[g]):
@@ -124,12 +124,38 @@
                 zcopies[g, kind, d] = put(wsh.at[:, here], zbuf[kind].at[z], zsem.at[g, i, d], at_z(d))
             zbuf[kind][z] = wsh[:, here]
 
+    z_near = [1] if Z == 2 else [1, 2, Z - 2, Z - 1]
+    last = []
+
+    def zv_start():
+        here = cols((2 + c) * D, D)
+        for i, d in enumerate(z_near):
+            zcopies[1, d] = put(wsh.at[:, here], zv.at[z], zsem.at[1, 0, i], at_z(d))
+        zv[z] = wsh[:, here]
+
+    def zv_forward():
+        for d in z_near:
+            zcopies[1, d].wait_recv()
+        if Z == 8:
+            behind, ahead = lax.rem(z + Z - 2, Z), lax.rem(z + 2, Z)
+            slot = jnp.where(c == 0, behind, ahead)
+            far = jnp.where(c == 0, ahead, behind)
+            last.append(put(zv.at[slot], zv.at[slot], zsem.at[1, 1, 0], {"z": far}))
+            last.append(put(zv.at[behind], zv.at[behind], zsem.at[1, 1, 1], at_z(1)))
+            last.append(put(zv.at[ahead], zv.at[ahead], zsem.at[1, 1, 2], at_z(Z - 1)))
+
+    def zv_last():
+        for copy in last:
+            copy.wait_recv()
+
     def x_start(g, kind):
         i = kinds[g].index(kind)
-        for d in range(1, Z):
-            zcopies[g, kind, d].wait_recv()
+        if g == 0:
+            for d in range(1, Z):
+                zcopies[g, kind, d].wait_recv()
         here = wcols(g, c, kind, y)
-        w[rows_of(0), here] = zbuf[kind][...].astype(F32).reshape(XR, wide[kind]).astype(BF16)
+        got = zbuf[kind][...] if g == 0 else zv[:, :, kind * 2 * LANES : (kind + 1) * 2 * LANES]
+        w[rows_of(0), here] = got.astype(F32).reshape(XR, wide[kind]).astype(BF16)
         own = w.at[rows_of(0), here]
         for j, d in enumerate(near_x):
             xcopies[g, kind, d] = put(own, own, xsem.at[g, i, j], at_x(d))
@@ -227,7 +253,7 @@
         return carry
 
     z_start(0)
-    z_start(1)
+    zv_start()
     loads[0].wait()
     lax.fori_loop(0, NP, normalise, 0)
     norm_copy = swap(norm_t.at[c], psem.at[0])
@@ -238,8 +264,8 @@
     for d in near_x:
         y_start(0, d)
     y_forward(0, 0)
+    zv_forward()
     x_forward(0, "a")
-    x_start(1, 0)
     x_last(0, "c")
     if X == 4:
         y_start(0, 2)
@@ -248,8 +274,9 @@
         y_forward(0, d)
     x_last(0, "a")
     hand_over(0, 0, "a")
-    x_start(1, 1)
-    x_start(1, 2)
+    zv_last()
+    for k in kinds[1]:
+        x_start(1, k)
     if X == 4:
         y_forward(0, 2)
     hand_near(0)
@@ -508,12 +535,22 @@
     sq[me, :1] = jnp.sum(sqz[:, :1], axis=0)
     line = sq.at[me, :1]
     sqs = [put(line, line, sqsem.at[i], at_cand(i % (Y * C)) | at_x(i // (Y * C))) for i in range(1, X * Y * C)]
+    for copy in started:
+        if all(copy is not v for v in (*sqs, norm_copy)):
+            copy.wait_send()
     for copy in sqs:
         copy.wait_recv()
     out_s[0] = jnp.max(jnp.sum(sq[:, :1], axis=0))
-    for copy in started:
-        if copy is not norm_copy:
-            copy.wait_send()
+    for copy in sqs:
+        copy.wait_send()
+
+
+def finish_kernel(count, summed, scalars, update, loss):
+    total = jnp.full((8, LANES), scalars[0], F32)
+    scale = (1.0 / (jnp.sqrt(total * (1.0 / count)) + EPS))[:1, :1]
+    update[...] = summed[...].astype(F32) * scale
+    for k in range(loss.shape[0]):
+        loss[k] = scalars[1 + k]
 
 
 def solution(mesh):
@@ -560,7 +597,7 @@
                 V((C, 3, NP, D), BF16),
                 V((Z, R, LANES), BF16),
                 V((Z, R, D - Y * LANES), BF16),
-                V((3, Z, R, 2 * LANES), BF16),
+                V((Z, R, D), BF16),
                 V((Y * C, 2, NP, LANES), F32),
                 V((PARTS, 2, HR // 2, NC), BF16),
                 V((PARTS, 2, X, HR // 2, NB), BF16),
@@ -598,8 +635,12 @@
             ],
             compiler_params=pltpu.CompilerParams(collective_id=0, has_side_effects=True, vmem_limit_bytes=60 * 2**20),
         )(hidden, attn_weight, norm_gain, pos_bias, score_weight, pair_lengths, labels)
-        scale = 1.0 / (jnp.sqrt(scalars[0] / (4.0 * D * D)) + EPS)
-        return summed.astype(F32) * scale, scalars[1:]
+        return pl.pallas_call(
+            functools.partial(finish_kernel, 4.0 * D * D),
+            out_shape=(jax.ShapeDtypeStruct((R, 4 * D), F32), jax.ShapeDtypeStruct((QL,), F32)),
+            in_specs=[vmem, smem],
+            out_specs=(vmem, smem),
+        )(summed, scalars)
 
     placed = (P(dp, cand, None, None), P(dp, None), P(), P(), P(), P(dp, cand), P(dp, cand))
     return jax.shard_map(shards, mesh=split, in_specs=placed, out_specs=(P(dp, None), P(dp)), check_vma=False)

time: 90.4 us -> 88.2 us (0.976)
  other arithmetic: 1.64 us -> 0 us
  Pallas kernels: 86 us -> 87.3 us
  local copies, waits for them, and re-layouts: 1.23 us -> 0 us
    pallas_call x0 -> x1, Pallas kernels: none -> 1.68 us  [shards(): pl.pallas_call(functools.partial(finish_kernel, 4.0 * D * D), out_shape=(...]
    mul x1 -> x0, other arithmetic: 1.64 us -> none  [shards(): return (summed.astype(F32) * scale, scalars[1:])]
    slice x1 -> x0, local copies, waits for them, and re-layouts: 1.23 us -> none  [shards(): return (summed.astype(F32) * scale, scalars[1:])]
where the time goes in v5:
time: 88.2 us; the launch traced here: 88.1 us
  Pallas kernels  87.3 us (99%)
    pallas_call x1, Pallas kernels, shards(): pl.pallas_call(functools.partial(step_kernel, (X, Z, Y, C)), out_shape=(j...  85.6 us

profile of v5, /device:TPU:1, one launch (start us, length us, event | category | flops | bytes accessed | tf_op | source)
XLA Modules:
  0.0 88.1 jit_solution(905763703224046769)
XLA Ops:
  0.6 85.6 %shard_map.86 = (bf16[24,3072]{1,0:T(8,128)(2,1)}, f32[3]{0:T(128)}) custom-call(bf16[2,4,128,768]{3,2,1,0:T(8,128)(2,1)} %hid_in.1, bf16[24,3072]{1,0:T(8,128)(2,1)} %wsh_in.1, f32[768]{0:T(1024)} %gain.1, f32[12,128,128]{2,1,0:T(8,128)} %bias_in.1, f32[768]{0:T(1024)} %sw.1, s32[2,4]{1,0:T(2,128)} %lens.1, s32[2,4]{1,0:T(2,128)} %labs.1), custom_call_target="tpu_custom_call" | custom-call | tf_op jit(solution)/shard_map/pallas_call | solution.py:573
  86.2 1.7 %shard_map.87 = (f32[24,3072]{1,0:T(8,128)}, f32[2]{0:T(128)}) custom-call(bf16[24,3072]{1,0:T(8,128)(2,1)} %get-tuple-element.4.summed, f32[3]{0:T(128)} %get-tuple-element.5.scalars), custom_call_target="tpu_custom_call" | custom-call | tf_op jit(solution)/shard_map/pallas_call | solution.py:638

commit v6 on v5

--- a/solution.py
+++ b/solution.py
@@ -448,6 +448,8 @@
             z3c[t, d].wait_recv()
             total += z3[t, d - 1].astype(F32)
         ob[t, cand] = total.astype(BF16)
+
+    def spread(t):
         for i in range(1, Y * C):
             obc[t, i] = put(ob.at[t, cand], ob.at[t, cand], obsem.at[t, i], at_cand(i))
 
@@ -505,7 +507,9 @@
     reduce_3(1)
     reduce_3(2)
     reduce_4(0)
+    spread(0)
     reduce_4(1)
+    spread(1)
     reduce_4(2)
     squares = jnp.zeros((R, NB), F32)
     for t in range(PARTS):
@@ -515,26 +519,31 @@
     sqz[z] = jnp.broadcast_to(squares, (8, LANES))
     zline = sqz.at[z, :1]
     zsq = [put(zline, zline, sqzsem.at[d], at_z(d)) for d in range(1, Z)]
-    for copy in obc.values():
-        copy.wait_recv()
-    for t in range(PARTS):
-        for k in range(Y * C):
-            for m in range(NB // LANES):
-                b, core = (t * NC + (k // C) * NB) // LANES + m, k % C
-                outer = DC // LANES
-                if b < outer:
-                    n = 3 * D + core * DC + b * LANES
-                elif b < 2 * outer:
-                    n = 2 * D + core * DC + (b - outer) * LANES
-                else:
-                    n = (b - 2 * outer) % 2 * D + (core * HC + (b - 2 * outer) // 2) * LANES
-                upd[:, n : n + LANES] = ob[t, k, :, m * LANES : (m + 1) * LANES]
+    spread(PARTS - 1)
+
+    def write_out():
+        for copy in obc.values():
+            copy.wait_recv()
+        for t in range(PARTS):
+            for k in range(Y * C):
+                for m in range(NB // LANES):
+                    b, core = (t * NC + (k // C) * NB) // LANES + m, k % C
+                    outer = DC // LANES
+                    if b < outer:
+                        n = 3 * D + core * DC + b * LANES
+                    elif b < 2 * outer:
+                        n = 2 * D + core * DC + (b - outer) * LANES
+                    else:
+                        n = (b - 2 * outer) % 2 * D + (core * HC + (b - 2 * outer) // 2) * LANES
+                    upd[:, n : n + LANES] = ob[t, k, :, m * LANES : (m + 1) * LANES]
+
     for copy in zsq:
         copy.wait_recv()
     me = x * Y * C + cand
     sq[me, :1] = jnp.sum(sqz[:, :1], axis=0)
     line = sq.at[me, :1]
     sqs = [put(line, line, sqsem.at[i], at_cand(i % (Y * C)) | at_x(i // (Y * C))) for i in range(1, X * Y * C)]
+    write_out()
     for copy in started:
         if all(copy is not v for v in (*sqs, norm_copy)):
             copy.wait_send()

time: 88.2 us -> 88.2 us (level)
  no operation moved by 1% of the time
where the time goes in v6:
time: 88.2 us; the launch traced here: 88 us
  Pallas kernels  87.2 us (99%)
    pallas_call x1, Pallas kernels, shards(): pl.pallas_call(functools.partial(step_kernel, (X, Z, Y, C)), out_shape=(j...  85.5 us

profile of v6, /device:TPU:1, one launch (start us, length us, event | category | flops | bytes accessed | tf_op | source)
XLA Modules:
  0.0 88.0 jit_solution(11452304789230019182)
XLA Ops:
  0.6 85.5 %shard_map.86 = (bf16[24,3072]{1,0:T(8,128)(2,1)}, f32[3]{0:T(128)}) custom-call(bf16[2,4,128,768]{3,2,1,0:T(8,128)(2,1)} %hid_in.1, bf16[24,3072]{1,0:T(8,128)(2,1)} %wsh_in.1, f32[768]{0:T(1024)} %gain.1, f32[12,128,128]{2,1,0:T(8,128)} %bias_in.1, f32[768]{0:T(1024)} %sw.1, s32[2,4]{1,0:T(2,128)} %lens.1, s32[2,4]{1,0:T(2,128)} %labs.1), custom_call_target="tpu_custom_call" | custom-call | tf_op jit(solution)/shard_map/pallas_call | solution.py:582
  86.2 1.7 %shard_map.87 = (f32[24,3072]{1,0:T(8,128)}, f32[2]{0:T(128)}) custom-call(bf16[24,3072]{1,0:T(8,128)(2,1)} %get-tuple-element.4.summed, f32[3]{0:T(128)} %get-tuple-element.5.scalars), custom_call_target="tpu_custom_call" | custom-call | tf_op jit(solution)/shard_map/pallas_call | solution.py:647
